TPU v7x, 32 devices: a 4x2x2 block of a 4x4x8 slice. The times are simulated.
32 devices in a mesh: dp: 4 (over y, z), sp: 8 (over x, core).
Axes of the slice: x: 4, y: 2, z: 2, core: 2. Of those that a mesh axis runs over, the one named last changes fastest.
The devices are a block of a 4x4x8 slice.
Arguments:
- images: float32 [24, 224, 224, 3], P('dp', 'sp'), parts along dimension 0
- w_patch: bfloat16 [14, 14, 3, 1152], replicated
- b_patch: float32 [1152], replicated
- pos_embed: bfloat16 [256, 1152], P('sp')
- ln1_gain: float32 [1152], replicated
- ln1_bias: float32 [1152], replicated
- w_qkv: bfloat16 [1152, 3, 16, 72], replicated
- b_qkv: float32 [3, 16, 72], replicated
- w_out: bfloat16 [16, 72, 1152], replicated
- b_out: float32 [1152], replicated
- ln2_gain: float32 [1152], replicated
- ln2_bias: float32 [1152], replicated
- w_fc1: bfloat16 [1152, 4304], replicated
- b_fc1: float32 [4304], replicated
- w_fc2: bfloat16 [4304, 1152], replicated
- b_fc2: float32 [1152], replicated
Outputs:
- output: bfloat16 [24, 256, 1152], P('dp', 'sp'), parts along dimension 0
There are 4 independent parts. A program takes and returns all parts, laid end to end along the dimension named above; an argument that names none is the same for every part.
All inputs are finite; a program needn't handle non-finite values.
Results may differ from a plain program's by a relative error of at most 0.0126451.
Values are sent between devices in bfloat16 or wider.
A program may use at most 768 MiB of HBM per device.

v0:
```python
import math
import jax
import jax.numpy as jnp
from jax import lax
from jax.sharding import PartitionSpec as P

LN_EPS = 1e-6


def layer_norm(x_in, ln_gain, ln_bias):
    row_mean = jnp.mean(x_in, axis=-1, keepdims=True)
    centered = x_in - row_mean
    variance = jnp.mean(centered * centered, axis=-1, keepdims=True)
    return centered * lax.rsqrt(variance + LN_EPS) * ln_gain + ln_bias


def embed_tokens(images, w_patch, b_patch, pos_embed):
    num_images, num_rows, num_cols, channels = images.shape
    patch_len = w_patch.shape[0]
    grid_rows = num_rows // patch_len
    grid_cols = num_cols // patch_len
    pixels = images.astype(jnp.bfloat16).reshape(num_images, grid_rows, patch_len, grid_cols, patch_len, channels)
    patch_embed = jnp.einsum('bypxqc,pqcd->byxd', pixels, w_patch, preferred_element_type=jnp.float32)
    patch_embed = patch_embed.reshape(num_images, grid_rows * grid_cols, w_patch.shape[3])
    return (patch_embed + b_patch + pos_embed.astype(jnp.float32)).astype(jnp.bfloat16)


def attend(queries, keys_all, values_all):
    num_images, n_query, num_heads, head_dim = queries.shape
    tile_len = math.gcd(n_query, 128)
    score_scale = head_dim ** -0.5

    def one_image(operands):
        q_img, k_img, v_img = operands

        def one_group(q_group):
            scores = jnp.einsum('qhe,khe->hqk', q_group, k_img, preferred_element_type=jnp.float32) * score_scale
            att_weights = jax.nn.softmax(scores, axis=-1).astype(jnp.bfloat16)
            return jnp.einsum('hqk,khe->qhe', att_weights, v_img, preferred_element_type=jnp.float32).astype(jnp.bfloat16)

        grouped = lax.map(one_group, q_img.reshape(n_query // tile_len, tile_len, num_heads, head_dim))
        return grouped.reshape(n_query, num_heads, head_dim)

    return lax.map(one_image, (queries, keys_all, values_all))


def finish_layer(x_zero, attended, w_out, b_out, ln2_gain, ln2_bias, w_fc1, b_fc1, w_fc2, b_fc2):
    residual = x_zero.astype(jnp.float32) + jnp.einsum('bnhe,hed->bnd', attended, w_out, preferred_element_type=jnp.float32) + b_out
    normed_two = layer_norm(residual, ln2_gain, ln2_bias).astype(jnp.bfloat16)
    hidden = jax.nn.gelu(jnp.einsum('bnd,df->bnf', normed_two, w_fc1, preferred_element_type=jnp.float32) + b_fc1, approximate=True).astype(jnp.bfloat16)
    return (residual + jnp.einsum('bnf,fd->bnd', hidden, w_fc2, preferred_element_type=jnp.float32) + b_fc2).astype(jnp.bfloat16)


def solution(mesh):
    def device_step(images, w_patch, b_patch, pos_embed, ln1_gain, ln1_bias, w_qkv, b_qkv, w_out, b_out, ln2_gain, ln2_bias, w_fc1, b_fc1, w_fc2, b_fc2):
        x_zero = embed_tokens(images, w_patch, b_patch, pos_embed)
        normed = layer_norm(x_zero.astype(jnp.float32), ln1_gain, ln1_bias).astype(jnp.bfloat16)
        qkv_proj = (jnp.einsum('bnd,dthe->bnthe', normed, w_qkv, preferred_element_type=jnp.float32) + b_qkv).astype(jnp.bfloat16)
        key_value = lax.all_gather(qkv_proj[:, :, 1:], 'sp', axis=1, tiled=True)
        attended = attend(qkv_proj[:, :, 0], key_value[:, :, 0], key_value[:, :, 1])
        return finish_layer(x_zero, attended, w_out, b_out, ln2_gain, ln2_bias, w_fc1, b_fc1, w_fc2, b_fc2)

    in_specs = (P('dp', 'sp', None, None), P(), P(), P('sp', None), P(), P(), P(), P(), P(), P(), P(), P(), P(), P(), P(), P())
    return jax.shard_map(device_step, mesh=mesh, in_specs=in_specs, out_specs=P('dp', 'sp', None), check_vma=False)
```

profile of v0, /device:TPU:81, one launch (start us, length us, event | category | flops | bytes accessed | tf_op | source)
XLA Modules:
  0.0 177.0 jit_solution(10770852261944979343)
XLA Ops:
  6.5 0.0 copy-start
  6.6 0.0 all-gather.2.cloned.1.call-start
  6.6 1.7 convert_element_type.40
  8.3 1.1 convert_element_type.39
  9.4 3.5 %reshape.43 = bf16[6,2,14,16,14,3]{4,3,2,1,5,0:T(8,128)(2,1)} reshape(bf16[6,28,224,3]{2,1,3,0:T(8,128)(2,1)S(1)} %convert_element_type.39) | data formatting | bytes 451584 | tf_op jit(solution)/shard_map/reshape | solution.py:22
  12.9 6.3 %copy.33 = bf16[6,2,16,3,14,14]{2,1,5,4,0,3:T(2,128)(2,1)} copy(bf16[6,2,16,3,14,14]{5,2,4,1,3,0:T(8,128)(2,1)} %bitcast.123) | data formatting | bytes 451584 | tf_op jit(solution)/shard_map/bypxqc,pqcd->byxd/dot_general | solution.py:23
  19.3 4.4 %reshape.52 = bf16[6,32,3,14,14]{1,4,3,0,2:T(8,128)(2,1)} reshape(bf16[6,2,16,3,14,14]{2,1,5,4,0,3:T(2,128)(2,1)} %copy.33) | data formatting | bytes 451584 | tf_op jit(solution)/shard_map/bypxqc,pqcd->byxd/dot_general | solution.py:23
  23.7 0.0 copy-done.2
  23.7 2.4 %fusion.102 = (f32[6,32]{1,0:T(8,128)S(1)}, f32[6,32,1152]{2,1,0:T(8,128)S(1)}) fusion(f32[32,1152]{1,0:T(8,128)} %convert_element_type.40, f32[1152]{0:T(1024)S(1)} %copy-done.2, bf16[6,32,3,14,14]{1,4,3,0,2:T(8,128)(2,1)} %reshape.52, bf16[14,14,3,1152]{3,1,2,0:T(8,128)(2,1)} %param.19), kind=kOutput, calls=%fused_computation.74 | convolution fusion | flops 261218112 | bytes 2618112 | tf_op jit(solution)/shard_map/bypxqc,pqcd->byxd/dot_general | solution.py:23
  26.1 0.2 multiply_reduce_fusion.1
  26.4 0.0 copy-done.5
  26.4 0.0 copy-done.3
  26.4 5.9 %add_convert_fusion = bf16[6,32,3,16,72]{4,1,3,2,0:T(8,128)(2,1)S(1)} fusion(f32[3,16,72]{2,1,0:T(8,128)S(1)} %copy-done.3, bf16[1152,3,16,72]{0,3,2,1:T(8,128)(2,1)} %param.24, f32[6,32,1152]{2,1,0:T(8,128)S(1)} %get-tuple-element.76, f32[1152]{0:T(1024)S(1)} %copy-done.5, f32[1152]{0:T(1024)S(1)} %copy-done.6, f32[6,32]{1,0:T(8,128)S(1)} %add_rsqrt_fusion.1, ...), kind=kOutput, calls=%fused_computation.32 | convolution fusion | flops 1531256832 | bytes 10199040 | tf_op jit(solution)/shard_map/bnd,dthe->bnthe/dot_general | solution.py:58
  32.3 1.4 copy-done.1
  33.7 1.4 slice.16
  35.1 0.1 all-gather.2.cloned.1.call-update
  35.2 2.1 %slice_bitcast_fusion.2 = bf16[6,32,16,72]{3,1,2,0:T(8,128)(2,1)} fusion(bf16[6,32,3,16,72]{4,1,3,2,0:T(8,128)(2,1)} %copy-done.1), kind=kLoop, calls=%fused_computation.59 | loop fusion | bytes 884736 | tf_op jit(solution)/shard_map/squeeze | solution.py:60
  37.4 66.8 %all-gather.2.cloned.1.call-done = bf16[6,256,2,16,72]{4,1,3,2,0:T(8,128)(2,1)} async-done(((bf16[6,32,2,16,72]{4,1,3,2,0:T(8,128)(2,1)}), bf16[6,256,2,16,72]{4,1,3,2,0:T(8,128)(2,1)}) %all-gather.2.cloned.1.call-update) | async-done | bytes 7077904 | tf_op jit(solution)/shard_map/all_gather | solution.py:59
  104.2 10.5 %slice_bitcast_fusion = (bf16[6,256,16,72]{3,1,2,0:T(8,128)(2,1)}, bf16[6,256,16,72]{3,1,2,0:T(8,128)(2,1)}) fusion(bf16[6,256,2,16,72]{4,1,3,2,0:T(8,128)(2,1)} %all-gather.2.cloned.1.call-done), kind=kLoop, calls=%fused_computation.29 | loop fusion | bytes 14155776 | tf_op jit(solution)/shard_map/squeeze | solution.py:60
  114.7 7.7 %copy.28 = bf16[6,256,16,72]{1,3,2,0:T(8,128)(2,1)} copy(bf16[6,256,16,72]{3,1,2,0:T(8,128)(2,1)} %get-tuple-element.73) | data formatting | bytes 7077888 | tf_op jit(solution)/shard_map/while | solution.py:44
  122.4 7.7 %copy.27 = bf16[6,256,16,72]{1,3,2,0:T(8,128)(2,1)} copy(bf16[6,256,16,72]{3,1,2,0:T(8,128)(2,1)} %get-tuple-element.74) | data formatting | bytes 7077888 | tf_op jit(solution)/shard_map/while | solution.py:44
  130.1 27.0 %while.10 = (s32[]{:T(128)}, bf16[6,32,16,72]{3,1,2,0:T(8,128)(2,1)}, bf16[6,256,16,72]{1,3,2,0:T(8,128)(2,1)}, bf16[6,32,16,72]{3,1,2,0:T(8,128)(2,1)}, bf16[6,256,16,72]{1,3,2,0:T(8,128)(2,1)}, /*index=5*/s32[]{:T(128)}) while((s32[]{:T(128)}, bf16[6,32,16,72]{3,1,2,0:T(8,128)(2,1)}, bf16[6,256,16,72]{1,3,2,0:T(8,128)(2,1)}, ...), condition=%wide.region_5.6_spmd, body=%wide.region_2.5_spmd.sunk | while | flops 57578496 | bytes 2169933 | solution.py:44
  130.1 1.6 fusion.120
  131.7 3.0 %fusion.121 = bf16[6,32,16,72]{3,1,2,0:T(8,128)(2,1)} fusion(bf16[6,32,16,72]{3,1,2,0:T(8,128)(2,1)} %get-tuple-element.117, s32[]{:T(128)S(6)} %copy.44, bf16[6,256,16,72]{1,3,2,0:T(8,128)(2,1)} %get-tuple-element.124, f32[16,32]{1,0:T(8,128)S(1)} %fusion.120, bf16[6,256,16,72]{1,3,2,0:T(8,128)(2,1)} %get-tuple-element.126, ...), kind=kOutput, calls=%fused_computation.6.clone.1 | convolution fusion | flops 38310656 | bytes 1445888 | tf_op jit(solution)/shard_map/while/body/eval_jaxpr/while/body/eval_jaxpr/hqk,khe->qhe/dot_general | solution.py:39
  134.6 1.5 fusion.120
  136.2 2.9 %fusion.121 = bf16[6,32,16,72]{3,1,2,0:T(8,128)(2,1)} fusion(bf16[6,32,16,72]{3,1,2,0:T(8,128)(2,1)} %get-tuple-element.117, s32[]{:T(128)S(6)} %copy.44, bf16[6,256,16,72]{1,3,2,0:T(8,128)(2,1)} %get-tuple-element.124, f32[16,32]{1,0:T(8,128)S(1)} %fusion.120, bf16[6,256,16,72]{1,3,2,0:T(8,128)(2,1)} %get-tuple-element.126, ...), kind=kOutput, calls=%fused_computation.6.clone.1 | convolution fusion | flops 38310656 | bytes 1445888 | tf_op jit(solution)/shard_map/while/body/eval_jaxpr/while/body/eval_jaxpr/hqk,khe->qhe/dot_general | solution.py:39
  139.1 1.5 fusion.120
  140.7 3.0 %fusion.121 = bf16[6,32,16,72]{3,1,2,0:T(8,128)(2,1)} fusion(bf16[6,32,16,72]{3,1,2,0:T(8,128)(2,1)} %get-tuple-element.117, s32[]{:T(128)S(6)} %copy.44, bf16[6,256,16,72]{1,3,2,0:T(8,128)(2,1)} %get-tuple-element.124, f32[16,32]{1,0:T(8,128)S(1)} %fusion.120, bf16[6,256,16,72]{1,3,2,0:T(8,128)(2,1)} %get-tuple-element.126, ...), kind=kOutput, calls=%fused_computation.6.clone.1 | convolution fusion | flops 38310656 | bytes 1445888 | tf_op jit(solution)/shard_map/while/body/eval_jaxpr/while/body/eval_jaxpr/hqk,khe->qhe/dot_general | solution.py:39
  143.6 1.5 fusion.120
  145.2 2.9 %fusion.121 = bf16[6,32,16,72]{3,1,2,0:T(8,128)(2,1)} fusion(bf16[6,32,16,72]{3,1,2,0:T(8,128)(2,1)} %get-tuple-element.117, s32[]{:T(128)S(6)} %copy.44, bf16[6,256,16,72]{1,3,2,0:T(8,128)(2,1)} %get-tuple-element.124, f32[16,32]{1,0:T(8,128)S(1)} %fusion.120, bf16[6,256,16,72]{1,3,2,0:T(8,128)(2,1)} %get-tuple-element.126, ...), kind=kOutput, calls=%fused_computation.6.clone.1 | convolution fusion | flops 38310656 | bytes 1445888 | tf_op jit(solution)/shard_map/while/body/eval_jaxpr/while/body/eval_jaxpr/hqk,khe->qhe/dot_general | solution.py:39
  148.1 1.5 fusion.120
  149.7 3.0 %fusion.121 = bf16[6,32,16,72]{3,1,2,0:T(8,128)(2,1)} fusion(bf16[6,32,16,72]{3,1,2,0:T(8,128)(2,1)} %get-tuple-element.117, s32[]{:T(128)S(6)} %copy.44, bf16[6,256,16,72]{1,3,2,0:T(8,128)(2,1)} %get-tuple-element.124, f32[16,32]{1,0:T(8,128)S(1)} %fusion.120, bf16[6,256,16,72]{1,3,2,0:T(8,128)(2,1)} %get-tuple-element.126, ...), kind=kOutput, calls=%fused_computation.6.clone.1 | convolution fusion | flops 38310656 | bytes 1445888 | tf_op jit(solution)/shard_map/while/body/eval_jaxpr/while/body/eval_jaxpr/hqk,khe->qhe/dot_general | solution.py:39
  152.6 1.5 fusion.120
  154.2 3.0 %fusion.121 = bf16[6,32,16,72]{3,1,2,0:T(8,128)(2,1)} fusion(bf16[6,32,16,72]{3,1,2,0:T(8,128)(2,1)} %get-tuple-element.117, s32[]{:T(128)S(6)} %copy.44, bf16[6,256,16,72]{1,3,2,0:T(8,128)(2,1)} %get-tuple-element.124, f32[16,32]{1,0:T(8,128)S(1)} %fusion.120, bf16[6,256,16,72]{1,3,2,0:T(8,128)(2,1)} %get-tuple-element.126, ...), kind=kOutput, calls=%fused_computation.6.clone.1 | convolution fusion | flops 38310656 | bytes 1445888 | tf_op jit(solution)/shard_map/while/body/eval_jaxpr/while/body/eval_jaxpr/hqk,khe->qhe/dot_general | solution.py:39
  157.2 0.0 copy-done
  157.2 0.0 copy-start.8
  157.2 0.0 copy-start.9
  157.2 0.0 slice-start
  157.2 2.2 %fusion.103 = (f32[6,32]{1,0:T(8,128)S(1)}, f32[6,32,1152]{2,1,0:T(8,128)S(1)}) fusion(f32[1152]{0:T(1024)S(1)} %copy-done.7, f32[6,32,1152]{2,1,0:T(8,128)S(1)} %get-tuple-element.76, bf16[6,32,16,72]{3,1,2,0:T(8,128)(2,1)} %get-tuple-element.47, bf16[16,72,1152]{2,1,0:T(8,128)(2,1)S(1)} %copy-done), kind=kOutput, calls=%fused_computation.75 | convolution fusion | flops 510271296 | bytes 4871424 | tf_op jit(solution)/shard_map/bnhe,hed->bnd/dot_general | solution.py:48
  159.5 0.2 multiply_reduce_fusion
  159.7 0.0 copy-done.4
  159.7 0.0 copy-done.8
  159.7 0.0 copy-done.9
  159.7 0.0 slice-start.1
  159.8 0.0 slice-start.2
  159.8 0.0 copy-start.10
  159.8 7.1 %fusion.57 = bf16[6,32,4304]{2,1,0:T(8,128)(2,1)S(1)} fusion(bf16[1152,4304]{0,1:T(8,128)(2,1)} %param.30, f32[4304]{0:T(1024)S(1)} %copy-done.4, f32[6,32,1152]{2,1,0:T(8,128)S(1)} %get-tuple-element.78, f32[1152]{0:T(1024)S(1)} %copy-done.8, f32[1152]{0:T(1024)S(1)} %copy-done.9, f32[6,32]{1,0:T(8,128)S(1)} %add_rsqrt_fusion, ...), kind=kOutput, calls=%fused_computation.40 | convolution fusion | flops 1913321472 | bytes 12481856 | tf_op jit(solution)/shard_map/bnd,df->bnf/dot_general | solution.py:50
  167.0 3.1 %fusion.81 = bf16[6,32,1152]{2,1,0:T(8,128)(2,1)} fusion(f32[6,32,1152]{2,1,0:T(8,128)S(1)} %get-tuple-element.78, bf16[6,32,4304]{2,1,0:T(8,128)(2,1)S(1)} %fusion.57, bf16[4304,1152]{1,0:T(8,128)(2,1)S(1)} %bitcast.125, f32[1152]{0:T(1024)S(1)} %copy-done.10), kind=kOutput, calls=%fused_computation.53 | convolution fusion | flops 1904615424 | bytes 12900864 | tf_op jit(solution)/shard_map/bnf,fd->bnd/dot_general | solution.py:51
  (19 shorter events, 0.0 us)
Async XLA Ops:
  6.5 150.6 %copy-start = (bf16[16,72,1152]{2,1,0:T(8,128)(2,1)S(1)}, bf16[16,72,1152]{2,1,0:T(8,128)(2,1)}, u32[]{:S(2)}) copy-start(bf16[16,72,1152]{2,1,0:T(8,128)(2,1)} %param.26) | copy-start | bytes 7962628
  6.6 97.6 %all-gather.2.cloned.1.call-start = ((), (), s32[]{:S(2)}) async-start(), calls=%async_computation | async-start | bytes 14155776 | tf_op jit(solution)/shard_map/all_gather | solution.py:59
  12.9 10.8 %copy-start.2 = (f32[1152]{0:T(1024)S(1)}, f32[1152]{0:T(1024)}, u32[]{:S(2)}) copy-start(f32[1152]{0:T(1024)} %param.20) | copy-start | bytes 13828
  19.3 7.1 %copy-start.5 = (f32[1152]{0:T(1024)S(1)}, f32[1152]{0:T(1024)}, u32[]{:S(2)}) copy-start(f32[1152]{0:T(1024)} %param.23) | copy-start | bytes 13828
  23.7 2.7 %copy-start.3 = (f32[3,16,72]{2,1,0:T(8,128)S(1)}, f32[3,16,72]{2,1,0:T(8,128)}, u32[]{:S(2)}) copy-start(f32[3,16,72]{2,1,0:T(8,128)} %param.25) | copy-start | bytes 41476
  23.7 2.7 %copy-start.6 = (f32[1152]{0:T(1024)S(1)}, f32[1152]{0:T(1024)}, u32[]{:S(2)}) copy-start(f32[1152]{0:T(1024)} %param.22) | copy-start | bytes 13828
  32.3 1.4 copy-start.1
  130.1 27.1 %copy-start.7 = (f32[1152]{0:T(1024)S(1)}, f32[1152]{0:T(1024)}, u32[]{:S(2)}) copy-start(f32[1152]{0:T(1024)} %param.27) | copy-start | bytes 13828
  157.2 2.5 %copy-start.4 = (f32[4304]{0:T(1024)S(1)}, f32[4304]{0:T(1024)}, u32[]{:S(2)}) copy-start(f32[4304]{0:T(1024)} %param.31) | copy-start | bytes 51652
  157.2 2.5 %copy-start.8 = (f32[1152]{0:T(1024)S(1)}, f32[1152]{0:T(1024)}, u32[]{:S(2)}) copy-start(f32[1152]{0:T(1024)} %param.29) | copy-start | bytes 13828
  157.2 2.5 %copy-start.9 = (f32[1152]{0:T(1024)S(1)}, f32[1152]{0:T(1024)}, u32[]{:S(2)}) copy-start(f32[1152]{0:T(1024)} %param.28) | copy-start | bytes 13828
  157.2 9.7 %slice-start = ((s8[9916416]{0:T(1024)(128)(4,1)}), s8[4194304]{0:T(1024)(128)(4,1)S(1)}, s32[]{:S(2)}) async-start(s8[9916416]{0:T(1024)(128)(4,1)} %bitcast.124), calls=%async_computation.1 | async-start | bytes 8388608
  159.7 7.2 %slice-start.1 = ((s8[9916416]{0:T(1024)(128)(4,1)}), s8[4194304]{0:T(1024)(128)(4,1)S(1)}, s32[]{:S(2)}) async-start(s8[9916416]{0:T(1024)(128)(4,1)} %bitcast.124), calls=%async_computation.2 | async-start | bytes 8388608
  159.8 7.2 %slice-start.2 = ((s8[9916416]{0:T(1024)(128)(4,1)}), s8[1527808]{0:T(1024)(128)(4,1)S(1)}, s32[]{:S(2)}) async-start(s8[9916416]{0:T(1024)(128)(4,1)} %bitcast.124), calls=%async_computation.3 | async-start | bytes 3055616
  159.8 7.2 %copy-start.10 = (f32[1152]{0:T(1024)S(1)}, f32[1152]{0:T(1024)}, u32[]{:S(2)}) copy-start(f32[1152]{0:T(1024)} %param.33) | copy-start | bytes 13828
Sparse Core Ops, SparseCore 0:
  35.3 68.7 all-gather.1
where the time goes:
time: 178 us; the launch traced here: 177 us
  waiting for transfers between devices  66.8 us (38%)
  matrix products  47.8 us (27%)
  local copies, waits for them, and re-layouts  45.3 us (25%)
  between operations  13.7 us (8%)
  other arithmetic  3.28 us (2%)
    all_gather x1, waiting for transfers between devices, device_step(): key_value = lax.all_gather(qkv_proj[:, :, 1:], 'sp', axis=1, tiled=True)  66.8 us
    dot_general x6, matrix products, one_group(): jnp.einsum('hqk,khe->qhe', att_weights, v_img, preferred_element_type=jnp...  17.7 us
    while x2, local copies, waits for them, and re-layouts, attend(): return lax.map(one_image, (queries, keys_all, values_all))  15.5 us
    squeeze x2, local copies, waits for them, and re-layouts, device_step(): attended = attend(qkv_proj[:, :, 0], key_value[:, :, 0], key_value[:, :, 1])  12.7 us
    dot_general x2, local copies, waits for them, and re-layouts, embed_tokens(): jnp.einsum('bypxqc,pqcd->byxd', pixels, w_patch, preferred_element_type=j...  10.8 us
    sub x6, matrix products, one_group(): att_weights = jax.nn.softmax(scores, axis=-1).astype(jnp.bfloat16)  9.28 us
    dot_general x1, matrix products, finish_layer(): jnp.einsum('bnd,df->bnf', normed_two, w_fc1, preferred_element_type=jnp.f...  7.15 us
    dot_general x1, matrix products, device_step(): jnp.einsum('bnd,dthe->bnthe', normed, w_qkv, preferred_element_type=jnp.f...  5.88 us
  transfers between devices with their start and end apart: 1, of which 1 were waited for; matrix products, arithmetic and copies ran while one was open for 1% of the time, Pallas kernels for 0%

commit v1 on v0

v1 whole, which is shorter than its diff:
```python
import functools
import math

import jax
import jax.numpy as jnp
from jax import lax
from jax.experimental import pallas as pl
from jax.experimental.pallas import tpu as pltpu
from jax.sharding import PartitionSpec as P

LN_EPS = 1e-6
F32 = jnp.float32
BF16 = jnp.bfloat16
NT = (((1,), (1,)), ((), ()))
NN = (((1,), (0,)), ((), ()))


def dot(a, b, dims=NN):
    return lax.dot_general(a, b, dims, preferred_element_type=F32)


def norm(z, gain, bias):
    mean = jnp.mean(z, axis=-1, keepdims=True)
    cen = z - mean
    var = jnp.mean(cen * cen, axis=-1, keepdims=True)
    return cen * lax.rsqrt(var + LN_EPS) * gain + bias


def gelu(x):
    inner = math.sqrt(2.0 / math.pi) * (x + 0.044715 * (x * x * x))
    return 0.5 * x * (1.0 + jnp.tanh(inner))


def chunk_transpose(w, chunk):
    rows, lanes = w.shape
    r = lax.broadcasted_iota(jnp.int32, w.shape, 0) % 8
    c = lax.broadcasted_iota(jnp.int32, w.shape, 1) // chunk
    for s in (4, 2, 1):
        up = pltpu.roll(pltpu.roll(w, s * chunk, 1), rows - s, 0)
        down = pltpu.roll(pltpu.roll(w, lanes - s * chunk, 1), s, 0)
        rb, cb = (r & s) != 0, (c & s) != 0
        w = jnp.where(rb == cb, w, jnp.where(cb, up, down))
    return w


def body(cfg, img_hbm, wp_hbm, bp, pos, g1, be1, wqkv_hbm, bqkv, wo_hbm, bo, g2, be2, w1_hbm, b1, w2_hbm, b2, out,
         img, wp_raw, wp, wqkv, wo, w1, w2, zf, xs, x0, y1, yrecv, kall, qt, vt, ot, osend, orecv, res, y2, acc, kbias,
         wsem, ssem, rsem, ossem, orsem):
    n, nimg, tok, d, heads, hd, ff, patch, chans = cfg
    ntok = n * tok
    per, own = 4, 3
    me = lax.axis_index('sp')
    half = nimg // 2

    def owner(i):
        return per * (i // own) + i % own

    cp_img = [pltpu.make_async_copy(img_hbm.at[pl.ds(half * k, half)], img.at[pl.ds(half * k, half)], wsem.at[k]) for k in range(2)]
    cp_wp = pltpu.make_async_copy(wp_hbm, wp_raw, wsem.at[2])
    cp_wqkv = pltpu.make_async_copy(wqkv_hbm, wqkv, wsem.at[3])
    cp_wo = pltpu.make_async_copy(wo_hbm, wo, wsem.at[4])
    cp_w1 = pltpu.make_async_copy(w1_hbm, w1, wsem.at[5])
    cp_w2 = pltpu.make_async_copy(w2_hbm, w2, wsem.at[6])
    cp_img[0].start()
    cp_img[1].start()
    cp_wp.start()
    barrier = pltpu.get_barrier_semaphore()
    for k in range(1, n):
        pl.semaphore_signal(barrier, inc=1, device_id={'sp': lax.rem(me + k, n)}, device_id_type=pl.DeviceIdType.MESH)

    zf[...] = jnp.zeros_like(zf)
    lrow = lax.broadcasted_iota(jnp.int32, (224, 256), 0)
    lcol = lax.broadcasted_iota(jnp.int32, (224, 256), 1)
    sel = jnp.where((lcol % 16 < patch) & (lrow == patch * (lcol // 16) + lcol % 16), 1.0, 0.0).astype(BF16)
    wp[...] = jnp.zeros_like(wp)

    rows_half = half * tok
    for k in range(2):
        cp_img[k].wait()
        if k == 0:
            cp_wqkv.start()
            cp_wo.start()
            cp_w1.start()
            cp_w2.start()
        for b in range(half):
            for y in range(2):
                for c in range(chans):
                    zf[(b * 2 + y) * chans + c, 0:patch, :] = img[half * k + b, c, patch * y:patch * y + patch, :]
        nz = half * 2 * chans
        u = dot(zf[...].reshape(nz * 16, 224).astype(BF16), sel)
        u = u.reshape(nz, 2, 8, 256)
        for ph in range(2):
            parts = []
            for xh in range(2):
                blk = u[:, ph, :, 128 * xh:128 * xh + 128].reshape(nz * 8, 128)
                parts.append(chunk_transpose(blk, 16).reshape(nz, 1, 8, 128))
            t = jnp.concatenate(parts, axis=1).reshape(half * 2, chans, 16, 128).astype(BF16)
            for c in range(chans):
                xs[pl.ds(rows_half * k, rows_half), 256 * c + 128 * ph:256 * c + 128 * ph + 128] = t[:, c].reshape(rows_half, 128)
        if k == 0:
            cp_wp.wait()
            for c in range(chans):
                for p in range(patch):
                    wp[c * 16 + p, 0:patch, :] = wp_raw[p * chans + c]
        e = dot(xs[pl.ds(rows_half * k, rows_half), :], wp[...].reshape(chans * 256, d))
        base = bp[...] + pos[...].astype(F32)
        e = e + jnp.concatenate([base] * half, axis=0)
        xb = e.astype(BF16)
        x0[pl.ds(rows_half * k, rows_half), :] = xb
        y1[pl.ds(rows_half * k, rows_half), :] = norm(xb.astype(F32), g1[...], be1[...]).astype(BF16)
        if k == 0:
            pl.semaphore_wait(barrier, n - 1)
        for i in range(half * k, half * k + half):
            o = owner(i)

            @pl.when(me != o)
            def _():
                pltpu.make_async_remote_copy(
                    y1.at[pl.ds(tok * i, tok)], yrecv.at[pl.ds(pl.multiple_of(tok * me, tok), tok)],
                    ssem.at[i], rsem.at[me], device_id={'sp': o}, device_id_type=pl.DeviceIdType.MESH).start()

            @pl.when(me == o)
            def _():
                yrecv[pl.ds(pl.multiple_of(tok * me, tok), tok), :] = y1[tok * i:tok * i + tok, :]

    img_idx = own * (me // per) + lax.rem(me, per)

    @pl.when(lax.rem(me, per) < own)
    def _():
        for k in range(1, n):
            s = lax.rem(me + k, n)
            pltpu.make_async_remote_copy(
                y1.at[pl.ds(0, tok)], yrecv.at[pl.ds(pl.multiple_of(tok * s, tok), tok)],
                ssem.at[0], rsem.at[s], device_id={'sp': s}, device_id_type=pl.DeviceIdType.MESH).wait_recv()
        cp_wqkv.wait()
        y = yrecv[...]
        for h in range(heads):
            kbias[0:1, hd * h:hd * h + hd] = bqkv[1, h:h + 1, :]
        for j in range(0, d, 256):
            w = min(256, d - j)
            kall[:, j:j + w] = (dot(y, wqkv[d + j:d + j + w, :], NT) + kbias[0:1, j:j + w]).astype(BF16)
        qbt = jnp.transpose(bqkv[0])
        vbt = jnp.transpose(bqkv[2])
        hh = heads // 2
        for a in range(2):
            qt[pl.ds(hd * hh * a, hd * hh), :] = dot(wqkv[hd * hh * a:hd * hh * a + hd * hh, :], y, NT)
            vt[pl.ds(hd * hh * a, hd * hh), :] = dot(wqkv[2 * d + hd * hh * a:2 * d + hd * hh * a + hd * hh, :], y, NT)
        scale = hd ** -0.5
        for h in range(heads):
            win = min(hd * h // 128 * 128, d - 256)
            off = hd * h - win
            q = qt[hd * h:hd * h + hd, :] + qbt[:, h:h + 1]
            pads = [jnp.zeros((k, ntok), F32) if k else None for k in (off, 256 - off - hd)]
            q = jnp.concatenate([z for z in (pads[0], q, pads[1]) if z is not None], axis=0).astype(BF16)
            s = dot(kall[:, win:win + 256], q) * scale
            m = jnp.max(s, axis=0, keepdims=True)
            p = jnp.exp(s - m)
            p = (p * (1.0 / jnp.sum(p, axis=0, keepdims=True))).astype(BF16)
            v = (vt[hd * h:hd * h + hd, :] + vbt[:, h:h + 1]).astype(BF16)
            ot[pl.ds(hd * h, hd), :] = dot(v, p)
        eye = jnp.where(lax.broadcasted_iota(jnp.int32, (ntok, ntok), 0) == lax.broadcasted_iota(jnp.int32, (ntok, ntok), 1),
                        1.0, 0.0).astype(BF16)
        for j in range(0, d, 256):
            w = min(256, d - j)
            osend[:, j:j + w] = dot(eye, ot[j:j + w, :].astype(BF16), NT).astype(BF16)
        for k in (4, 5, 3, 2, 6, 7, 1):
            s = lax.rem(me + k, n)
            pltpu.make_async_remote_copy(
                osend.at[pl.ds(pl.multiple_of(tok * s, tok), tok)], orecv.at[pl.ds(pl.multiple_of(tok * img_idx, tok), tok)],
                ossem.at[s], orsem.at[img_idx], device_id={'sp': s}, device_id_type=pl.DeviceIdType.MESH).start()
        orecv[pl.ds(pl.multiple_of(tok * img_idx, tok), tok), :] = osend[pl.ds(pl.multiple_of(tok * me, tok), tok), :]

    @pl.when(lax.rem(me, per) >= own)
    def _():
        cp_wqkv.wait()

    for i in range(nimg):
        o = owner(i)

        @pl.when(me != o)
        def _():
            pltpu.make_async_remote_copy(
                osend.at[pl.ds(0, tok)], orecv.at[pl.ds(tok * i, tok)],
                ossem.at[0], orsem.at[i], device_id={'sp': o}, device_id_type=pl.DeviceIdType.MESH).wait_recv()

    cp_wo.wait()
    r = x0[...].astype(F32) + dot(orecv[...], wo[...]) + bo[...]
    res[...] = r
    y2[...] = norm(r, g2[...], be2[...]).astype(BF16)
    cp_w1.wait()
    cp_w2.wait()
    step = 512
    full = ff // step
    acc[...] = jnp.zeros_like(acc)

    def mlp(start, size):
        h = dot(y2[...], w1[pl.ds(start, size), :], NT) + b1[:, pl.ds(start, size)]
        acc[...] += dot(gelu(h).astype(BF16), w2[pl.ds(start, size), :])

    def mlp_step(c, carry):
        mlp(pl.multiple_of(c * step, step), step)
        return carry

    lax.fori_loop(0, full, mlp_step, 0)
    mlp(full * step, ff - full * step)
    out[...] = (res[...] + acc[...] + b2[...]).astype(BF16)

    for i in range(nimg):
        o = owner(i)

        @pl.when(me != o)
        def _():
            pltpu.make_async_remote_copy(
                y1.at[pl.ds(tok * i, tok)], yrecv.at[pl.ds(0, tok)],
                ssem.at[i], rsem.at[0], device_id={'sp': o}, device_id_type=pl.DeviceIdType.MESH).wait_send()

    @pl.when(lax.rem(me, per) < own)
    def _():
        for k in range(1, n):
            s = lax.rem(me + k, n)
            pltpu.make_async_remote_copy(
                osend.at[pl.ds(0, tok)], orecv.at[pl.ds(0, tok)],
                ossem.at[s], orsem.at[0], device_id={'sp': s}, device_id_type=pl.DeviceIdType.MESH).wait_send()


def solution(mesh):
    n = mesh.shape['sp']

    def device_step(images, w_patch, b_patch, pos_embed, ln1_gain, ln1_bias, w_qkv, b_qkv, w_out, b_out, ln2_gain, ln2_bias, w_fc1, b_fc1, w_fc2, b_fc2):
        nimg, rows, width, chans = images.shape
        tok, d = pos_embed.shape
        patch = w_patch.shape[0]
        _, _, heads, hd = w_qkv.shape
        ff = w_fc1.shape[1]
        m = nimg * tok
        cfg = (n, nimg, tok, d, heads, hd, ff, patch, chans)
        img_t = jnp.transpose(images, (0, 3, 1, 2))
        wp_t = jnp.transpose(w_patch, (0, 2, 1, 3)).reshape(patch * chans, patch, d)
        wqkv_t = jnp.transpose(w_qkv, (1, 2, 3, 0)).reshape(3 * d, d)
        wo_t = w_out.reshape(d, d)
        w1_t = jnp.transpose(w_fc1, (1, 0))

        def row(v):
            return v.reshape(1, -1)

        hbm = pl.BlockSpec(memory_space=pl.ANY)
        vm = pl.BlockSpec(memory_space=pltpu.VMEM)
        V = pltpu.VMEM
        half = nimg // 2
        out = pl.pallas_call(
            functools.partial(body, cfg),
            out_shape=jax.ShapeDtypeStruct((m, d), BF16),
            in_specs=[hbm, hbm, vm, vm, vm, vm, hbm, vm, hbm, vm, vm, vm, hbm, vm, hbm, vm],
            out_specs=vm,
            scratch_shapes=[
                V(img_t.shape, F32), V((patch * chans, patch, d), BF16), V((chans * 16, 16, d), BF16),
                V((3 * d, d), BF16), V((d, d), BF16), V((ff, d), BF16), V((ff, d), BF16),
                V((half * 2 * chans, 16, width), F32), V((m, chans * 256), BF16),
                V((m, d), BF16), V((m, d), BF16), V((n * tok, d), BF16),
                V((n * tok, d), BF16), V((d, n * tok), F32), V((d, n * tok), F32), V((d, n * tok), F32),
                V((n * tok, d), BF16), V((m, d), BF16), V((m, d), F32), V((m, d), BF16), V((m, d), F32), V((1, d), F32),
                pltpu.SemaphoreType.DMA((7,)), pltpu.SemaphoreType.DMA((nimg,)), pltpu.SemaphoreType.DMA((n,)),
                pltpu.SemaphoreType.DMA((n,)), pltpu.SemaphoreType.DMA((nimg,)),
            ],
            compiler_params=pltpu.CompilerParams(collective_id=0, has_side_effects=True, vmem_limit_bytes=64 * 1024 * 1024 - 128 * 1024),
            name='siglip_layer',
        )(img_t, wp_t, row(b_patch), pos_embed, row(ln1_gain), row(ln1_bias), wqkv_t, b_qkv, wo_t, row(b_out),
          row(ln2_gain), row(ln2_bias), w1_t, row(b_fc1), w_fc2, row(b_fc2))
        return out.reshape(nimg, tok, d)

    in_specs = (P('dp', 'sp', None, None), P(), P(), P('sp', None), P(), P(), P(), P(), P(), P(), P(), P(), P(), P(), P(), P())
    return jax.shard_map(device_step, mesh=mesh, in_specs=in_specs, out_specs=P('dp', 'sp', None), check_vma=False)
```

time: 178 us -> 51.7 us (0.29)
  waiting for transfers between devices: 66.8 us -> 0 us
  matrix products: 47.8 us -> 0 us
  Pallas kernels: 0 us -> 38.9 us
  local copies, waits for them, and re-layouts: 45.3 us -> 12.2 us
  between operations: 13.7 us -> 0.01 us
  other arithmetic: 3.28 us -> 0 us
    all_gather x1 -> x0, waiting for transfers between devices: 66.8 us -> none  [device_step(): key_value = lax.all_gather(qkv_proj[:, :, 1:], 'sp', axis=1, tiled=True)]
    pallas_call x0 -> x1, Pallas kernels: none -> 38.9 us  [device_step(): pl.pallas_call(functools.partial(body, cfg), out_shape=jax.ShapeDtypeStru...]
    dot_general x11 -> x0, matrix products: 38.5 us -> none  [the longest x6 17.7 us: one_group(): jnp.einsum('hqk,khe->qhe', att_weights, v_img, preferred_element_type=jnp...]
    while x2 -> x0, local copies, waits for them, and re-layouts: 15.5 us -> none  [attend(): return lax.map(one_image, (queries, keys_all, values_all))]
    squeeze x2 -> x0, local copies, waits for them, and re-layouts: 12.7 us -> none  [device_step(): attended = attend(qkv_proj[:, :, 0], key_value[:, :, 0], key_value[:, :, 1])]
    dot_general x2 -> x0, local copies, waits for them, and re-layouts: 10.8 us -> none  [embed_tokens(): jnp.einsum('bypxqc,pqcd->byxd', pixels, w_patch, preferred_element_type=j...]
    sub x6 -> x0, matrix products: 9.28 us -> none  [one_group(): att_weights = jax.nn.softmax(scores, axis=-1).astype(jnp.bfloat16)]
    reshape x1 -> x8, local copies, waits for them, and re-layouts: 3.55 us -> 10.4 us  [row(): return v.reshape(1, -1)]
  transfers between devices with their start and end apart: 1 -> 0, of which waited for: 1 -> 0; matrix products, arithmetic and copies ran while one was open for 1% -> 0% of each run, Pallas kernels for 0% -> 0%
where the time goes in v1:
time: 51.7 us; the launch traced here: 51.1 us
  Pallas kernels  38.9 us (75%)
  local copies, waits for them, and re-layouts  12.2 us (24%)
    pallas_call x1, Pallas kernels, device_step(): pl.pallas_call(functools.partial(body, cfg), out_shape=jax.ShapeDtypeStru...  38.9 us
    reshape x8, local copies, waits for them, and re-layouts, row(): return v.reshape(1, -1)  10.4 us
    unnamed x1, local copies, waits for them, and re-layouts  1.81 us

profile of v1, /device:TPU:81, one launch (start us, length us, event | category | flops | bytes accessed | tf_op | source)
XLA Modules:
  0.0 51.1 jit_solution(12948533023650441599)
XLA Ops:
  0.0 1.3 %reshape.37.bp = f32[1,1152]{1,0:T(1,128)} reshape(f32[1152]{0:T(1024)} %param.18) | data formatting | bytes 9216 | tf_op jit(solution)/shard_map/reshape | solution.py:244
  1.3 1.3 %reshape.38.g1 = f32[1,1152]{1,0:T(1,128)} reshape(f32[1152]{0:T(1024)} %param.20) | data formatting | bytes 9216 | tf_op jit(solution)/shard_map/reshape | solution.py:244
  2.6 1.3 %reshape.39.be1 = f32[1,1152]{1,0:T(1,128)} reshape(f32[1152]{0:T(1024)} %param.21) | data formatting | bytes 9216 | tf_op jit(solution)/shard_map/reshape | solution.py:244
  3.9 1.3 %reshape.42.bo = f32[1,1152]{1,0:T(1,128)} reshape(f32[1152]{0:T(1024)} %param.25) | data formatting | bytes 9216 | tf_op jit(solution)/shard_map/reshape | solution.py:244
  5.2 1.3 %reshape.43.g2 = f32[1,1152]{1,0:T(1,128)} reshape(f32[1152]{0:T(1024)} %param.26) | data formatting | bytes 9216 | tf_op jit(solution)/shard_map/reshape | solution.py:244
  6.4 1.3 %reshape.44.be2 = f32[1,1152]{1,0:T(1,128)} reshape(f32[1152]{0:T(1024)} %param.27) | data formatting | bytes 9216 | tf_op jit(solution)/shard_map/reshape | solution.py:244
  7.7 1.3 %reshape.46.b2 = f32[1,1152]{1,0:T(1,128)} reshape(f32[1152]{0:T(1024)} %param.31) | data formatting | bytes 9216 | tf_op jit(solution)/shard_map/reshape | solution.py:244
  9.0 1.3 %reshape.45.b1 = f32[1,4304]{1,0:T(1,128)} reshape(f32[4304]{0:T(1024)} %param.29) | data formatting | bytes 34432 | tf_op jit(solution)/shard_map/reshape | solution.py:244
  10.4 38.9 %siglip_layer.1 = bf16[192,1152]{1,0:T(8,128)(2,1)} custom-call(f32[6,3,28,224]{3,2,1,0:T(8,128)} %bitcast.15, bf16[42,14,1152]{2,1,0:T(8,128)(2,1)} %bitcast.14, f32[1,1152]{1,0:T(1,128)} %reshape.37.bp, bf16[32,1152]{1,0:T(8,128)(2,1)} %pos.1, f32[1,1152]{1,0:T(1,128)} %reshape.38.g1, f32[1,1152]{1,0:T(1,128)} %reshape.39.be1, ...), custom_call_target="tpu_custom_call" | custom-call | tf_op jit(solution)/shard_map/siglip_layer/pallas_call | solution.py:250
  49.3 1.8 %copy.18 = bf16[6,32,1152]{2,1,0:T(8,128)(2,1)} copy(bf16[6,32,1152]{2,1,0:T(8,128)(2,1)} %bitcast.13) | data formatting | bytes 884736

commit v2 on v1

--- a/solution.py
+++ b/solution.py
@@ -11,12 +11,17 @@
 LN_EPS = 1e-6
 F32 = jnp.float32
 BF16 = jnp.bfloat16
+LOG2E = 1.4426950408889634
 NT = (((1,), (1,)), ((), ()))
 NN = (((1,), (0,)), ((), ()))
 
 
 def dot(a, b, dims=NN):
     return lax.dot_general(a, b, dims, preferred_element_type=F32)
+
+
+def row(v):
+    return v[...].reshape(1, v.shape[0])
 
 
 def norm(z, gain, bias):
@@ -44,7 +49,7 @@
 
 
 def body(cfg, img_hbm, wp_hbm, bp, pos, g1, be1, wqkv_hbm, bqkv, wo_hbm, bo, g2, be2, w1_hbm, b1, w2_hbm, b2, out,
-         img, wp_raw, wp, wqkv, wo, w1, w2, zf, xs, x0, y1, yrecv, kall, qt, vt, ot, osend, orecv, res, y2, acc, kbias,
+         img, wp_raw, wp, wqkv, wo, w1, w2, zf, xs, x0, y1, yrecv, kall, qt, vt, ot, osend, orecv, res, y2, hid, kbias, sbuf, pbuf,
          wsem, ssem, rsem, ossem, orsem):
     n, nimg, tok, d, heads, hd, ff, patch, chans = cfg
     ntok = n * tok
@@ -103,11 +108,11 @@
                 for p in range(patch):
                     wp[c * 16 + p, 0:patch, :] = wp_raw[p * chans + c]
         e = dot(xs[pl.ds(rows_half * k, rows_half), :], wp[...].reshape(chans * 256, d))
-        base = bp[...] + pos[...].astype(F32)
+        base = row(bp) + pos[...].astype(F32)
         e = e + jnp.concatenate([base] * half, axis=0)
         xb = e.astype(BF16)
         x0[pl.ds(rows_half * k, rows_half), :] = xb
-        y1[pl.ds(rows_half * k, rows_half), :] = norm(xb.astype(F32), g1[...], be1[...]).astype(BF16)
+        y1[pl.ds(rows_half * k, rows_half), :] = norm(xb.astype(F32), row(g1), row(be1)).astype(BF16)
         if k == 0:
             pl.semaphore_wait(barrier, n - 1)
         for i in range(half * k, half * k + half):
@@ -145,19 +150,32 @@
         for a in range(2):
             qt[pl.ds(hd * hh * a, hd * hh), :] = dot(wqkv[hd * hh * a:hd * hh * a + hd * hh, :], y, NT)
             vt[pl.ds(hd * hh * a, hd * hh), :] = dot(wqkv[2 * d + hd * hh * a:2 * d + hd * hh * a + hd * hh, :], y, NT)
-        scale = hd ** -0.5
-        for h in range(heads):
+        ntile = 4
+
+        def scores(h):
             win = min(hd * h // 128 * 128, d - 256)
             off = hd * h - win
+            pads = [jnp.zeros((k, ntok), F32) if k else None for k in (off, 256 - off - hd)]
             q = qt[hd * h:hd * h + hd, :] + qbt[:, h:h + 1]
-            pads = [jnp.zeros((k, ntok), F32) if k else None for k in (off, 256 - off - hd)]
             q = jnp.concatenate([z for z in (pads[0], q, pads[1]) if z is not None], axis=0).astype(BF16)
-            s = dot(kall[:, win:win + 256], q) * scale
-            m = jnp.max(s, axis=0, keepdims=True)
-            p = jnp.exp(s - m)
-            p = (p * (1.0 / jnp.sum(p, axis=0, keepdims=True))).astype(BF16)
+            sbuf[h % ntile] = dot(kall[:, win:win + 256], q)
+
+        def soft(h):
+            for b in range(0, ntok, 128):
+                s = sbuf[h % ntile, :, b:b + 128]
+                m = jnp.max(s, axis=0, keepdims=True)
+                p = jnp.exp2((s - m) * (hd ** -0.5 * LOG2E))
+                pbuf[h % ntile, :, b:b + 128] = (p * (1.0 / jnp.sum(p, axis=0, keepdims=True))).astype(BF16)
+
+        def mix(h):
             v = (vt[hd * h:hd * h + hd, :] + vbt[:, h:h + 1]).astype(BF16)
-            ot[pl.ds(hd * h, hd), :] = dot(v, p)
+            ot[pl.ds(hd * h, hd), :] = dot(v, pbuf[h % ntile])
+
+        for g in range(0, heads + 4, 2):
+            for stage, lag in ((scores, 0), (soft, 2), (mix, 4)):
+                for h in range(g - lag, g - lag + 2):
+                    if 0 <= h < heads:
+                        stage(h)
         eye = jnp.where(lax.broadcasted_iota(jnp.int32, (ntok, ntok), 0) == lax.broadcasted_iota(jnp.int32, (ntok, ntok), 1),
                         1.0, 0.0).astype(BF16)
         for j in range(0, d, 256):
@@ -184,26 +202,20 @@
                 ossem.at[0], orsem.at[i], device_id={'sp': o}, device_id_type=pl.DeviceIdType.MESH).wait_recv()
 
     cp_wo.wait()
-    r = x0[...].astype(F32) + dot(orecv[...], wo[...]) + bo[...]
+    r = x0[...].astype(F32) + dot(orecv[...], wo[...]) + row(bo)
     res[...] = r
-    y2[...] = norm(r, g2[...], be2[...]).astype(BF16)
+    y2[...] = norm(r, row(g2), row(be2)).astype(BF16)
     cp_w1.wait()
     cp_w2.wait()
     step = 512
-    full = ff // step
-    acc[...] = jnp.zeros_like(acc)
-
-    def mlp(start, size):
-        h = dot(y2[...], w1[pl.ds(start, size), :], NT) + b1[:, pl.ds(start, size)]
-        acc[...] += dot(gelu(h).astype(BF16), w2[pl.ds(start, size), :])
-
-    def mlp_step(c, carry):
-        mlp(pl.multiple_of(c * step, step), step)
-        return carry
-
-    lax.fori_loop(0, full, mlp_step, 0)
-    mlp(full * step, ff - full * step)
-    out[...] = (res[...] + acc[...] + b2[...]).astype(BF16)
+    for c in range(0, ff, step):
+        w = min(step, ff - c)
+        h = dot(y2[...], w1[c:c + w, :], NT) + b1[pl.ds(c, w)].reshape(1, w)
+        hid[:, c:c + w] = gelu(h).astype(BF16)
+    for j in range(0, d, 256):
+        w = min(256, d - j)
+        acc = res[:, j:j + w] + dot(hid[...], w2[:, j:j + w])
+        out[:, j:j + w] = (acc + b2[pl.ds(j, w)].reshape(1, w)).astype(BF16)
 
     for i in range(nimg):
         o = owner(i)
@@ -239,9 +251,6 @@
         wqkv_t = jnp.transpose(w_qkv, (1, 2, 3, 0)).reshape(3 * d, d)
         wo_t = w_out.reshape(d, d)
         w1_t = jnp.transpose(w_fc1, (1, 0))
-
-        def row(v):
-            return v.reshape(1, -1)
 
         hbm = pl.BlockSpec(memory_space=pl.ANY)
         vm = pl.BlockSpec(memory_space=pltpu.VMEM)
@@ -258,14 +267,15 @@
                 V((half * 2 * chans, 16, width), F32), V((m, chans * 256), BF16),
                 V((m, d), BF16), V((m, d), BF16), V((n * tok, d), BF16),
                 V((n * tok, d), BF16), V((d, n * tok), F32), V((d, n * tok), F32), V((d, n * tok), F32),
-                V((n * tok, d), BF16), V((m, d), BF16), V((m, d), F32), V((m, d), BF16), V((m, d), F32), V((1, d), F32),
+                V((n * tok, d), BF16), V((m, d), BF16), V((m, d), F32), V((m, d), BF16), V((m, ff), BF16), V((1, d), F32),
+                V((4, n * tok, n * tok), F32), V((4, n * tok, n * tok), BF16),
                 pltpu.SemaphoreType.DMA((7,)), pltpu.SemaphoreType.DMA((nimg,)), pltpu.SemaphoreType.DMA((n,)),
                 pltpu.SemaphoreType.DMA((n,)), pltpu.SemaphoreType.DMA((nimg,)),
             ],
             compiler_params=pltpu.CompilerParams(collective_id=0, has_side_effects=True, vmem_limit_bytes=64 * 1024 * 1024 - 128 * 1024),
             name='siglip_layer',
-        )(img_t, wp_t, row(b_patch), pos_embed, row(ln1_gain), row(ln1_bias), wqkv_t, b_qkv, wo_t, row(b_out),
-          row(ln2_gain), row(ln2_bias), w1_t, row(b_fc1), w_fc2, row(b_fc2))
+        )(img_t, wp_t, b_patch, pos_embed, ln1_gain, ln1_bias, wqkv_t, b_qkv, wo_t, b_out,
+          ln2_gain, ln2_bias, w1_t, b_fc1, w_fc2, b_fc2)
         return out.reshape(nimg, tok, d)
 
     in_specs = (P('dp', 'sp', None, None), P(), P(), P('sp', None), P(), P(), P(), P(), P(), P(), P(), P(), P(), P(), P(), P())

time: 51.7 us -> 34.5 us (0.67)
  local copies, waits for them, and re-layouts: 12.2 us -> 1.81 us
  Pallas kernels: 38.9 us -> 32.4 us
    reshape x8 -> x0, local copies, waits for them, and re-layouts: 10.4 us -> none  [row(): return v.reshape(1, -1)]
    pallas_call x1, Pallas kernels: 38.9 us -> 32.4 us  [device_step(): pl.pallas_call(functools.partial(body, cfg), out_shape=jax.ShapeDtypeStru...]
where the time goes in v2:
time: 34.5 us; the launch traced here: 34.2 us
  Pallas kernels  32.4 us (94%)
  local copies, waits for them, and re-layouts  1.81 us (5%)
    pallas_call x1, Pallas kernels, device_step(): pl.pallas_call(functools.partial(body, cfg), out_shape=jax.ShapeDtypeStru...  32.4 us
    unnamed x1, local copies, waits for them, and re-layouts  1.81 us

profile of v2, /device:TPU:81, one launch (start us, length us, event | category | flops | bytes accessed | tf_op | source)
XLA Modules:
  0.0 34.2 jit_solution(5153396469606109857)
XLA Ops:
  0.0 32.4 %siglip_layer.1 = bf16[192,1152]{1,0:T(8,128)(2,1)} custom-call(f32[6,3,28,224]{3,2,1,0:T(8,128)} %bitcast.15, bf16[42,14,1152]{2,1,0:T(8,128)(2,1)} %bitcast.14, f32[1152]{0:T(1024)} %bp.1, bf16[32,1152]{1,0:T(8,128)(2,1)} %pos.1, f32[1152]{0:T(1024)} %g1.1, f32[1152]{0:T(1024)} %be1.1, bf16[3456,1152]{1,0:T(8,128)(2,1)} %bitcast.11, f32[3,16,72]{2,1,0:T(8,128)} %bqkv.1, ...), custom_call_target="tpu_custom_call" | custom-call | tf_op jit(solution)/shard_map/siglip_layer/pallas_call | solution.py:259
  32.4 1.8 %copy.18 = bf16[6,32,1152]{2,1,0:T(8,128)(2,1)} copy(bf16[6,32,1152]{2,1,0:T(8,128)(2,1)} %bitcast.13) | data formatting | bytes 884736

commit v3 on v2

v3 whole, which is shorter than its diff:
```python
import functools
import math

import jax
import jax.numpy as jnp
from jax import lax
from jax.experimental import pallas as pl
from jax.experimental.pallas import tpu as pltpu
from jax.sharding import PartitionSpec as P

LN_EPS = 1e-6
LOG2E = 1.4426950408889634
F32 = jnp.float32
BF16 = jnp.bfloat16
NT = (((1,), (1,)), ((), ()))
NN = (((1,), (0,)), ((), ()))
MESH = pl.DeviceIdType.MESH


def dot(a, b, dims=NN):
    return lax.dot_general(a, b, dims, preferred_element_type=F32)


def row(v):
    return v[...].reshape(1, v.shape[0])


def norm(z, gain, bias):
    mean = jnp.mean(z, axis=-1, keepdims=True)
    cen = z - mean
    var = jnp.mean(cen * cen, axis=-1, keepdims=True)
    return cen * lax.rsqrt(var + LN_EPS) * gain + bias


def gelu(x):
    inner = math.sqrt(2.0 / math.pi) * (x + 0.044715 * (x * x * x))
    return 0.5 * x * (1.0 + jnp.tanh(inner))


def chunk_transpose(w, chunk):
    rows, lanes = w.shape
    r = lax.broadcasted_iota(jnp.int32, w.shape, 0) % 8
    c = lax.broadcasted_iota(jnp.int32, w.shape, 1) // chunk
    for s in (4, 2, 1):
        up = pltpu.roll(pltpu.roll(w, s * chunk, 1), rows - s, 0)
        down = pltpu.roll(pltpu.roll(w, lanes - s * chunk, 1), s, 0)
        rb, cb = (r & s) != 0, (c & s) != 0
        w = jnp.where(rb == cb, w, jnp.where(cb, up, down))
    return w


def pack_heads(heads):
    out = []
    shape = (heads[0].shape[0], 128)
    lane = lax.broadcasted_iota(jnp.int32, shape, 1)
    upper, odd = lane >= 64, (lane // 32) % 2 == 1
    for t in range(0, heads[0].shape[1], 128):
        a = [x[:, t:t + 128] for x in heads]
        b = [None] * 4
        for j in (0, 1):
            b[j] = jnp.where(upper, pltpu.roll(a[j + 2], 64, 1), a[j])
            b[j + 2] = jnp.where(upper, a[j + 2], pltpu.roll(a[j], 64, 1))
        for j in (0, 2):
            out.append(jnp.where(odd, pltpu.roll(b[j + 1], 32, 1), b[j]))
            out.append(jnp.where(odd, b[j + 1], pltpu.roll(b[j], 96, 1)))
    return out


def body(cfg, *refs):
    n, nimg, tok, d, heads, hd, ff, patch, chans = cfg
    (img_hbm, wp_hbm, bp_h, pos_h, g1_h, be1_h, wqkv_hbm, bqkv_h, wo_hbm, bo_h, g2_h, be2_h, w1_hbm, b1_h, w2_hbm, b2_h, out,
     img, wp_raw, wp, wq, wo, w1, w2, bp, pos, g1, be1, bqkv, bo, g2, be2, b1, b2,
     zf, xs, x0, y1, yrecv, qkv, sbuf, pbuf, bsc, bcol, osend, orecv, og, res, y2, hid,
     isem, wsem, qsem, vsem, ssem, rsem, fsem, frsem, ossem, orsem) = refs
    ntok = n * tok
    gh, ng = 4, 3
    gw = gh * hd
    me = lax.axis_index('sp')
    chip, core = me // 2, lax.rem(me, 2)
    pair, side = chip // 2, lax.rem(chip, 2)
    img_full, img_split = 3 * pair + 2 * side, 3 * pair + 1

    def image_of(e):
        return 3 * (e // 4) + (e % 4 if e % 4 < 3 else 1)

    def source_of(i, hg):
        if i % 3 == 1:
            return 2 * (2 * (i // 3) + hg // 2) + 1
        return 2 * (2 * (i // 3) + (i % 3) // 2) + (1 if hg == 0 else 0)

    def send_y(i, src_row, e, slot):
        return pltpu.make_async_remote_copy(
            y1.at[pl.ds(src_row, tok)], yrecv.at[0, pl.ds(pl.multiple_of(tok * slot, tok), tok)],
            ssem.at[i], rsem.at[slot], device_id={'sp': e}, device_id_type=MESH)

    def forward(s, dst):
        rows = pl.ds(pl.multiple_of(tok * s, tok), tok)
        return pltpu.make_async_remote_copy(
            yrecv.at[0, rows], yrecv.at[1, rows], fsem.at[s], frsem.at[s], device_id={'sp': dst}, device_id_type=MESH)

    def send_o(g, s, hg, i):
        return pltpu.make_async_remote_copy(
            osend.at[g, s], orecv.at[hg, i], ossem.at[g, s], orsem.at[hg, i], device_id={'sp': s}, device_id_type=MESH)

    def head_group(g):
        if g < 2:
            return (1 - core) * (g + 1) + core * (2 * side + g)
        return (1 - core) * 3

    batches = ([i for i in range(nimg) if i % 3 == 1], [i for i in range(nimg) if i % 3 != 1])
    cp_img = [pltpu.make_async_copy(img_hbm.at[i], img.at[i], isem.at[i]) for i in range(nimg)]
    cp_wp = pltpu.make_async_copy(wp_hbm, wp_raw, wsem.at[0])
    cp_wo = pltpu.make_async_copy(wo_hbm, wo, wsem.at[1])
    cp_w1 = pltpu.make_async_copy(w1_hbm, w1, wsem.at[2])
    cp_w2 = pltpu.make_async_copy(w2_hbm, w2, wsem.at[3])
    cp_q = [pltpu.make_async_copy(
        wqkv_hbm.at[pl.ds(pl.multiple_of(d * t + gw * head_group(g), 32), gw)], wq.at[g, pl.ds(gw * t, gw)], qsem.at[g, t])
        for g in range(ng) for t in range(3)]
    cp_v = [pltpu.make_async_copy(a, b, vsem.at[k]) for k, (a, b) in enumerate(
        ((bp_h, bp), (pos_h, pos), (g1_h, g1), (be1_h, be1), (bqkv_h, bqkv), (bo_h, bo), (g2_h, g2), (be2_h, be2), (b1_h, b1), (b2_h, b2)))]
    for i in batches[0] + batches[1]:
        cp_img[i].start()
    cp_wp.start()
    for c in cp_v:
        c.start()
    barrier = pltpu.get_barrier_semaphore()
    for k in range(1, n):
        pl.semaphore_signal(barrier, inc=1, device_id={'sp': lax.rem(me + k, n)}, device_id_type=MESH)

    zf[...] = jnp.zeros_like(zf)
    lrow = lax.broadcasted_iota(jnp.int32, (224, 256), 0)
    lcol = lax.broadcasted_iota(jnp.int32, (224, 256), 1)
    sel = jnp.where((lcol % 16 < patch) & (lrow == patch * (lcol // 16) + lcol % 16), 1.0, 0.0).astype(BF16)
    wp[...] = jnp.zeros_like(wp)

    for bi, batch in enumerate(batches):
        nb = len(batch)
        for i in batch:
            cp_img[i].wait()
        if bi == len(batches) - 1:
            for c in cp_q:
                c.start()
            cp_wo.start()
            cp_w1.start()
            cp_w2.start()
        for b, i in enumerate(batch):
            for y in range(2):
                for c in range(chans):
                    zf[(b * 2 + y) * chans + c, 0:patch, :] = img[i, c, patch * y:patch * y + patch, :]
        nz = nb * 2 * chans
        u = dot(zf[0:nz].reshape(nz * 16, 224).astype(BF16), sel)
        u = u.reshape(nz, 2, 8, 256)
        for ph in range(2):
            parts = []
            for xh in range(2):
                blk = u[:, ph, :, 128 * xh:128 * xh + 128].reshape(nz * 8, 128)
                parts.append(chunk_transpose(blk, 16).reshape(nz, 1, 8, 128))
            t = jnp.concatenate(parts, axis=1).reshape(nb * 2, chans, 16, 128).astype(BF16)
            for c in range(chans):
                xs[0:nb * tok, 256 * c + 128 * ph:256 * c + 128 * ph + 128] = t[:, c].reshape(nb * tok, 128)
        if bi == 0:
            cp_wp.wait()
            for c in cp_v:
                c.wait()
            for c in range(chans):
                for p in range(patch):
                    wp[c * 16 + p, 0:patch, :] = wp_raw[p * chans + c]
        e = dot(xs[0:nb * tok, :], wp[...].reshape(chans * 256, d))
        base = row(bp) + pos[...].astype(F32)
        xb = (e + jnp.concatenate([base] * nb, axis=0)).astype(BF16)
        yb = norm(xb.astype(F32), row(g1), row(be1)).astype(BF16)
        for b, i in enumerate(batch):
            x0[tok * i:tok * i + tok, :] = xb[tok * b:tok * b + tok, :]
            y1[tok * i:tok * i + tok, :] = yb[tok * b:tok * b + tok, :]
        if bi == 0:
            pl.semaphore_wait(barrier, n - 1)
        for e in range(n):
            i = image_of(e)
            if i not in batch:
                continue

            @pl.when(me != e)
            def _():
                send_y(e, tok * i, e, me).start()

            @pl.when(me == e)
            def _():
                yrecv[0, pl.ds(pl.multiple_of(tok * me, tok), tok), :] = y1[tok * i:tok * i + tok, :]

    for t in range(3):
        for hg in range(heads // gh):
            bsc[t, hg, 0:gh, :] = bqkv[t, gh * hg:gh * hg + gh, :]
    for g in range(ng):
        for t in range(3):
            bcol[g, t] = jnp.transpose(bsc[t, head_group(g)])
    res[...] = x0[...].astype(F32) + row(bo)

    def project(g, slot, parts):
        for t in parts:
            qkv[g % 2, gw * t:gw * t + gw, :] = dot(wq[g, gw * t:gw * t + gw, :], yrecv[slot], NT)

    def head(g, t, j):
        return qkv[g % 2, gw * t + hd * j:gw * t + hd * j + hd, :] + bcol[g, t, :, j:j + 1]

    def scores(g, j):
        sbuf[j] = dot(jnp.transpose(head(g, 1, j)).astype(BF16), head(g, 0, j).astype(BF16))

    def soft(j):
        for b in range(0, ntok, 128):
            s = sbuf[j, :, b:b + 128]
            p = jnp.exp2((s - jnp.max(s, axis=0, keepdims=True)) * (hd ** -0.5 * LOG2E))
            pbuf[j, :, b:b + 128] = (p * (1.0 / jnp.sum(p, axis=0, keepdims=True))).astype(BF16)

    def mix(g, j):
        return dot(head(g, 2, j).astype(BF16), pbuf[j])

    def run_groups(gs, slot, i):
        for t in range(3):
            cp_q[3 * gs[0] + t].wait()
        project(gs[0], slot, range(3))
        for g in gs:
            if g + 1 in gs:
                for t in range(3):
                    cp_q[3 * (g + 1) + t].wait()
            for j in range(gh):
                scores(g, j)
            outs = []
            for j in range(gh):
                if g + 1 in gs and j < 3:
                    project(g + 1, slot, (j,))
                soft(j)
                if j:
                    outs.append(mix(g, j - 1))
            outs.append(mix(g, gh - 1))
            for e, o in enumerate(pack_heads(outs)):
                osend[g, e] = o.astype(BF16)
            hg = head_group(g)
            for k in (4, 5, 3, 2, 6, 7, 1):
                send_o(g, lax.rem(me + k, n), hg, i).start()
            orecv[hg, i] = osend[g, me]


    @pl.when(core == 0)
    def _():
        for k in (0, 1, 2, 3, 6, 7, 4, 5):
            s = lax.rem(me + k, n)
            if k:
                send_y(0, 0, s, s).wait_recv()
            forward(s, me + 1).start()
        run_groups((0, 1, 2), 0, img_full)

    @pl.when(core == 1)
    def _():
        for k in range(1, n):
            s = lax.rem(me + k, n)
            send_y(0, 0, s, s).wait_recv()
        run_groups((0, 1), 0, img_split)
        for s in range(n):
            forward(s, me - 1).wait_recv()
        run_groups((2,), 1, img_full)

    cp_wo.wait()
    for hg in (1, 0, 2, 3):
        for i in range(nimg):
            src = source_of(i, hg)

            @pl.when(me != src)
            def _():
                send_o(0, src, hg, i).wait_recv()
        for i in range(nimg):
            t = jnp.transpose(orecv[hg, i].astype(F32))
            for j in range(gh):
                og[tok * i:tok * i + tok, hd * j:hd * j + hd] = t[tok * j:tok * j + tok, :]
        res[...] += dot(og[...].astype(BF16), wo[gw * hg:gw * hg + gw, :])

    y2[...] = norm(res[...], row(g2), row(be2)).astype(BF16)
    cp_w1.wait()
    cp_w2.wait()
    step = 512
    for c in range(0, ff, step):
        w = min(step, ff - c)
        h = dot(y2[...], w1[c:c + w, :], NT) + b1[pl.ds(c, w)].reshape(1, w)
        hid[:, c:c + w] = gelu(h).astype(BF16)
    for j in range(0, d, 256):
        w = min(256, d - j)
        acc = res[:, j:j + w] + dot(hid[...], w2[:, j:j + w])
        out[:, j:j + w] = (acc + b2[pl.ds(j, w)].reshape(1, w)).astype(BF16)
    for e in range(n):
        @pl.when(me != e)
        def _():
            send_y(e, 0, e, 0).wait_send()

    @pl.when(core == 0)
    def _():
        for s in range(n):
            forward(s, me + 1).wait_send()

    for g in range(ng):
        for k in range(1, n):
            s = lax.rem(me + k, n)
            send_o(g, s, 0, 0).wait_send()


def solution(mesh):
    n = mesh.shape['sp']

    def device_step(images, w_patch, b_patch, pos_embed, ln1_gain, ln1_bias, w_qkv, b_qkv, w_out, b_out, ln2_gain, ln2_bias, w_fc1, b_fc1, w_fc2, b_fc2):
        nimg, rows, width, chans = images.shape
        tok, d = pos_embed.shape
        patch = w_patch.shape[0]
        _, _, heads, hd = w_qkv.shape
        ff = w_fc1.shape[1]
        m = nimg * tok
        ntok = n * tok
        cfg = (n, nimg, tok, d, heads, hd, ff, patch, chans)
        img_t = jnp.transpose(images, (0, 3, 1, 2))
        wp_t = jnp.transpose(w_patch, (0, 2, 1, 3)).reshape(patch * chans, patch, d)
        wqkv_t = jnp.transpose(w_qkv, (1, 2, 3, 0)).reshape(3 * d, d)
        wo_t = w_out.reshape(d, d)
        w1_t = jnp.transpose(w_fc1, (1, 0))

        hbm = pl.BlockSpec(memory_space=pl.ANY)
        V, S = pltpu.VMEM, pltpu.SemaphoreType.DMA
        out = pl.pallas_call(
            functools.partial(body, cfg),
            out_shape=jax.ShapeDtypeStruct((m, d), BF16),
            in_specs=[hbm] * 16,
            out_specs=pl.BlockSpec(memory_space=pltpu.VMEM),
            scratch_shapes=[
                V(img_t.shape, F32), V((patch * chans, patch, d), BF16), V((chans * 16, 16, d), BF16),
                V((3, 12 * hd, d), BF16), V((d, d), BF16), V((ff, d), BF16), V((ff, d), BF16),
                V((d,), F32), V((tok, d), BF16), V((d,), F32), V((d,), F32), V((3, heads, hd), F32), V((d,), F32), V((d,), F32),
                V((d,), F32), V((ff,), F32), V((d,), F32),
                V((8 * chans, 16, width), F32), V((4 * tok, chans * 256), BF16),
                V((m, d), BF16), V((m, d), BF16), V((2, ntok, d), BF16),
                V((2, 12 * hd, ntok), F32), V((4, ntok, ntok), F32), V((4, ntok, ntok), BF16),
                V((3, 4, 8, hd), F32), V((3, 3, hd, 8), F32),
                V((3, n, hd, 128), BF16), V((4, nimg, hd, 128), BF16), V((m, 4 * hd), F32), V((m, d), F32), V((m, d), BF16), V((m, ff), BF16),
                S((nimg,)), S((4,)), S((3, 3)), S((10,)), S((n,)), S((n,)), S((n,)), S((n,)), S((3, n)), S((4, nimg)),
            ],
            compiler_params=pltpu.CompilerParams(collective_id=0, has_side_effects=True, vmem_limit_bytes=64 * 1024 * 1024 - 128 * 1024),
            name='siglip_layer',
        )(img_t, wp_t, b_patch, pos_embed, ln1_gain, ln1_bias, wqkv_t, b_qkv, wo_t, b_out,
          ln2_gain, ln2_bias, w1_t, b_fc1, w_fc2, b_fc2)
        return out.reshape(nimg, tok, d)

    in_specs = (P('dp', 'sp', None, None), P(), P(), P('sp', None), P(), P(), P(), P(), P(), P(), P(), P(), P(), P(), P(), P())
    return jax.shard_map(device_step, mesh=mesh, in_specs=in_specs, out_specs=P('dp', 'sp', None), check_vma=False)
```

time: 34.5 us -> 33 us (0.957)
  Pallas kernels: 32.4 us -> 31 us
    pallas_call x1, Pallas kernels: 32.4 us -> 31 us  [device_step(): pl.pallas_call(functools.partial(body, cfg), out_shape=jax.ShapeDtypeStru...]
where the time goes in v3:
time: 33 us; the launch traced here: 32.8 us
  Pallas kernels  31 us (94%)
  local copies, waits for them, and re-layouts  1.81 us (5%)
    pallas_call x1, Pallas kernels, device_step(): pl.pallas_call(functools.partial(body, cfg), out_shape=jax.ShapeDtypeStru...  31 us
    unnamed x1, local copies, waits for them, and re-layouts  1.81 us

profile of v3, /device:TPU:81, one launch (start us, length us, event | category | flops | bytes accessed | tf_op | source)
XLA Modules:
  0.0 32.8 jit_solution(7029607823719170248)
XLA Ops:
  0.0 31.0 %siglip_layer.1 = bf16[192,1152]{1,0:T(8,128)(2,1)} custom-call(f32[6,3,28,224]{3,2,1,0:T(8,128)} %bitcast.15, bf16[42,14,1152]{2,1,0:T(8,128)(2,1)} %bitcast.14, f32[1152]{0:T(1024)} %refs_2_.1, bf16[32,1152]{1,0:T(8,128)(2,1)} %refs_3_.1, f32[1152]{0:T(1024)} %refs_4_.1, f32[1152]{0:T(1024)} %refs_5_.1, bf16[3456,1152]{1,0:T(8,128)(2,1)} %bitcast.11, ...), custom_call_target="tpu_custom_call" | custom-call | tf_op jit(solution)/shard_map/siglip_layer/pallas_call | solution.py:324
  31.0 1.8 %copy.18 = bf16[6,32,1152]{2,1,0:T(8,128)(2,1)} copy(bf16[6,32,1152]{2,1,0:T(8,128)(2,1)} %bitcast.13) | data formatting | bytes 884736

commit v4 on v3

v4 whole, which is shorter than its diff:
```python
import functools
import math

import jax
import jax.numpy as jnp
from jax import lax
from jax.experimental import pallas as pl
from jax.experimental.pallas import tpu as pltpu
from jax.sharding import PartitionSpec as P

LN_EPS = 1e-6
LOG2E = 1.4426950408889634
F32 = jnp.float32
BF16 = jnp.bfloat16
NT = (((1,), (1,)), ((), ()))
NN = (((1,), (0,)), ((), ()))
MESH = pl.DeviceIdType.MESH


def dot(a, b, dims=NN):
    return lax.dot_general(a, b, dims, preferred_element_type=F32)


def row(v):
    return v[...].reshape(1, v.shape[0])


def norm(z, gain, bias):
    mean = jnp.mean(z, axis=-1, keepdims=True)
    cen = z - mean
    var = jnp.mean(cen * cen, axis=-1, keepdims=True)
    return cen * lax.rsqrt(var + LN_EPS) * gain + bias


def gelu(x):
    inner = math.sqrt(2.0 / math.pi) * (x + 0.044715 * (x * x * x))
    return 0.5 * x * (1.0 + jnp.tanh(inner))


def chunk_transpose(w, chunk):
    rows, lanes = w.shape
    r = lax.broadcasted_iota(jnp.int32, w.shape, 0) % 8
    c = lax.broadcasted_iota(jnp.int32, w.shape, 1) // chunk
    for s in (4, 2, 1):
        up = pltpu.roll(pltpu.roll(w, s * chunk, 1), rows - s, 0)
        down = pltpu.roll(pltpu.roll(w, lanes - s * chunk, 1), s, 0)
        rb, cb = (r & s) != 0, (c & s) != 0
        w = jnp.where(rb == cb, w, jnp.where(cb, up, down))
    return w


def body(cfg, *refs):
    n, nimg, tok, d, heads, hd, ff, patch, chans = cfg
    (img_hbm, wp_hbm, bp_h, pos_h, g1_h, be1_h, wqkv_hbm, bqkv_h, wo_hbm, bo_h, g2_h, be2_h, w1_hbm, b1_h, w2_hbm, b2_h, out_hbm, out,
     img, wp_raw, wp, wq, wo, w1s, w1t, w2, bp, pos, g1, be1, bqkv, bo, g2, be2, b1, b2,
     zf, xs, x0, y1, yrecv, qkv, sbuf, pbuf, bsc, bcol, osend, orecv, res, y2, hid,
     outsem, isem, wsem, psem, qsem, csem, vsem, ssem, rsem, fsem, frsem, ossem, orsem) = refs
    ntok = n * tok
    gh, ng = 4, 4
    step, slots = w1s.shape[1], w1s.shape[0]
    gw = gh * hd
    me = lax.axis_index('sp')
    chip, core = me // 2, lax.rem(me, 2)
    pair, side = chip // 2, lax.rem(chip, 2)
    nxt = lax.rem(me + 1, n)
    pos_split, pos_full = pair, 2 + chip
    order = [i for i in range(nimg) if i % 3 == 1] + [i for i in range(nimg) if i % 3 != 1]

    def source_of(p, hg):
        return 2 * (2 * p + hg // 2) + 1 if p < 2 else 2 * (p - 2) + hg // 2

    def send_y(i, src_row, e, slot):
        return pltpu.make_async_remote_copy(
            y1.at[pl.ds(src_row, tok)], yrecv.at[0, pl.ds(pl.multiple_of(tok * slot, tok), tok)],
            ssem.at[i], rsem.at[slot], device_id={'sp': e}, device_id_type=MESH)

    def wait_sent(bi):
        for here in range(2):
            rows = pl.ds(0, tok * (n // 2 - (here != bi)))

            @pl.when(core == here)
            def _():
                pltpu.make_async_remote_copy(
                    yrecv.at[0, rows], yrecv.at[1, rows], ssem.at[bi], rsem.at[0], device_id={'sp': nxt}, device_id_type=MESH).wait_send()

    def forward(s, dst):
        rows = pl.ds(pl.multiple_of(tok * s, tok), tok)
        return pltpu.make_async_remote_copy(
            yrecv.at[0, rows], yrecv.at[1, rows], fsem.at[0], frsem.at[0], device_id={'sp': dst}, device_id_type=MESH)

    def forward_all(dst):
        return pltpu.make_async_remote_copy(
            yrecv.at[0], yrecv.at[1], fsem.at[0], frsem.at[0], device_id={'sp': dst}, device_id_type=MESH)

    def wave_of(g):
        return 1 - core if g < 2 else 1

    def send_o(g, s, hg, i):
        return pltpu.make_async_remote_copy(
            osend.at[g, pl.ds(pl.multiple_of(tok * s, tok), tok)], orecv.at[hg, pl.ds(pl.multiple_of(tok * i, tok), tok)],
            ossem.at[g], orsem.at[hg, wave_of(g)], device_id={'sp': s}, device_id_type=MESH)

    def head_group(g):
        return (1 - core) * g + core * (2 * side + g) if g < 2 else g

    def w1_copy(c, slot, size):
        start = c * step if isinstance(c, int) else pl.multiple_of(c * step, step)
        return pltpu.make_async_copy(w1_hbm.at[pl.ds(start, size)], w1s.at[slot, pl.ds(0, size)], csem.at[slot])

    batches = (order[:2], order[2:])
    bounds = (0, 2, nimg)
    cp_img = [pltpu.make_async_copy(img_hbm.at[i], img.at[i], isem.at[0 if i in order[:2] else 1]) for i in range(nimg)]
    cp_wp = [pltpu.make_async_copy(wp_hbm, wp_raw, psem.at[0])]
    cp_wo = pltpu.make_async_copy(wo_hbm, wo, wsem.at[0])
    cp_w2 = pltpu.make_async_copy(w2_hbm, w2, wsem.at[1])
    cp_q = [pltpu.make_async_copy(
        wqkv_hbm.at[pl.ds(pl.multiple_of(d * t + gw * head_group(g), 32), gw)], wq.at[g, pl.ds(gw * t, gw)], qsem.at[g])
        for g in range(ng) for t in range(3)]
    cp_v = [pltpu.make_async_copy(a, b, vsem.at[k]) for k, (a, b) in enumerate(
        ((bp_h, bp), (pos_h, pos), (g1_h, g1), (be1_h, be1), (bqkv_h, bqkv), (bo_h, bo), (g2_h, g2), (be2_h, be2), (b1_h, b1), (b2_h, b2)))]
    for c in cp_wp + [cp_img[i] for i in batches[0]] + cp_v[:4] + [cp_img[i] for i in batches[1]] + cp_v[4:]:
        c.start()
    wp[...] = jnp.zeros_like(wp)
    barrier = pltpu.get_barrier_semaphore()
    for k in range(1, n):
        pl.semaphore_signal(barrier, inc=1, device_id={'sp': lax.rem(me + k, n)}, device_id_type=MESH)

    zf[...] = jnp.zeros_like(zf)
    lrow = lax.broadcasted_iota(jnp.int32, (224, 256), 0)
    lcol = lax.broadcasted_iota(jnp.int32, (224, 256), 1)
    sel = jnp.where((lcol % 16 < patch) & (lrow == patch * (lcol // 16) + lcol % 16), 1.0, 0.0).astype(BF16)

    full, early = ff // step, 3
    rest = ff - full * step

    def turn(c, size, slot):
        w1t[:, pl.ds(c * step if isinstance(c, int) else pl.multiple_of(c * step, step), size)] = jnp.transpose(w1s[slot, 0:size])

    def turn_step(c, carry):
        slot = lax.rem(c, slots)
        w1_copy(c, slot, step).wait()
        turn(c, step, slot)

        @pl.when(c + slots < full)
        def _():
            w1_copy(c + slots, slot, step).start()

        @pl.when(c + slots == full)
        def _():
            w1_copy(full, slot, rest).start()

        return carry

    for bi, batch in enumerate(batches):
        nb = len(batch)
        pltpu.make_async_copy(img_hbm.at[pl.ds(0, nb)], img.at[pl.ds(0, nb)], isem.at[bi]).wait()
        if bi == len(batches) - 1:
            for c in cp_q[:6]:
                c.start()
        for b, i in enumerate(batch):
            for y in range(2):
                for c in range(chans):
                    zf[(b * 2 + y) * chans + c, 0:patch, :] = img[i, c, patch * y:patch * y + patch, :]
        nz = nb * 2 * chans
        u = dot(zf[0:nz].reshape(nz * 16, 224).astype(BF16), sel)
        u = u.reshape(nz, 2, 8, 256)
        for ph in range(2):
            parts = []
            for xh in range(2):
                blk = u[:, ph, :, 128 * xh:128 * xh + 128].reshape(nz * 8, 128)
                parts.append(chunk_transpose(blk, 16).reshape(nz, 1, 8, 128))
            t = jnp.concatenate(parts, axis=1).reshape(nb * 2, chans, 16, 128).astype(BF16)
            for c in range(chans):
                xs[0:nb * tok, 256 * c + 128 * ph:256 * c + 128 * ph + 128] = t[:, c].reshape(nb * tok, 128)
        if bi == 0:
            for c in cp_wp + cp_v[:4]:
                c.wait()
            for c in range(slots):
                w1_copy(c, c, step).start()
            for c in range(chans):
                for p in range(patch):
                    wp[c, p, 0:patch, :] = wp_raw[p, c]
        e = dot(xs[0:nb * tok, :], wp[...].reshape(chans * 256, d))
        base = row(bp) + pos[...].astype(F32)
        xb = (e + jnp.concatenate([base] * nb, axis=0)).astype(BF16)
        yb = norm(xb.astype(F32), row(g1), row(be1)).astype(BF16)
        x0[tok * bounds[bi]:tok * bounds[bi + 1], :] = xb
        y1[tok * bounds[bi]:tok * bounds[bi + 1], :] = yb
        if bi == 0:
            pl.semaphore_wait(barrier, n - 1)
        if bi == 1:
            lax.fori_loop(0, early, turn_step, 0)
            wait_sent(0)
        for k in (2, 1, 3, 0):
            c = lax.rem(chip + k, n // 2)
            if bi == 0:
                e, p = 2 * c + 1, c // 2
            else:
                e, p = 2 * c, 2 + c
            src = pl.multiple_of(tok * p, tok)

            @pl.when(me != e)
            def _():
                send_y(bi, src, e, me).start()

            @pl.when(me == e)
            def _():
                yrecv[0, pl.ds(pl.multiple_of(tok * me, tok), tok), :] = y1[pl.ds(src, tok), :]

    for c in cp_v[4:]:
        c.wait()
    for t in range(3):
        for hg in range(heads // gh):
            bsc[t, hg, 0:gh, :] = bqkv[t, gh * hg:gh * hg + gh, :]
    for g in range(ng):
        for t in range(3):
            bcol[g, t] = jnp.transpose(bsc[t, head_group(g)])
    res[...] = x0[...].astype(F32) + row(bo)
    lax.fori_loop(early, full, turn_step, 0)

    @pl.when(core == 1)
    def _():
        for c in cp_q[6:]:
            c.start()

    cp_wo.start()
    cp_w2.start()
    w1_copy(full, full % slots, rest).wait()
    turn(full, rest, full % slots)

    def project(g, slot, parts):
        for t in parts:
            qkv[g % 2, gw * t:gw * t + gw, :] = dot(wq[g, gw * t:gw * t + gw, :], yrecv[slot], NT)

    def head(g, t, j):
        return qkv[g % 2, gw * t + hd * j:gw * t + hd * j + hd, :] + bcol[g, t, :, j:j + 1]

    def scores(g, j):
        sbuf[j] = dot(jnp.transpose(head(g, 1, j)).astype(BF16), head(g, 0, j).astype(BF16))

    def soft(j):
        for b in range(0, ntok, 128):
            s = sbuf[j, :, b:b + 128]
            p = jnp.exp2((s - jnp.max(s, axis=0, keepdims=True)) * (hd ** -0.5 * LOG2E))
            pbuf[j, :, b:b + 128] = (p * (1.0 / jnp.sum(p, axis=0, keepdims=True))).astype(BF16)

    def mix(g, j):
        return dot(head(g, 2, j).astype(BF16), pbuf[j])

    def wait_q(g):
        pltpu.make_async_copy(wqkv_hbm.at[pl.ds(0, 3 * gw)], wq.at[g], qsem.at[g]).wait()

    def run_groups(gs, slot, i):
        wait_q(gs[0])
        project(gs[0], slot, range(3))
        for g in gs:
            if g + 1 in gs:
                wait_q(g + 1)
            for j in range(gh):
                scores(g, j)
            outs = []
            for j in range(gh):
                if g + 1 in gs and j < 3:
                    project(g + 1, slot, (j,))
                soft(j)
                if j:
                    outs.append(mix(g, j - 1))
            outs.append(mix(g, gh - 1))
            osend[g] = jnp.transpose(jnp.concatenate(outs, axis=0)).astype(BF16)
            hg = head_group(g)
            for k in (4, 5, 3, 2, 6, 7, 1):
                send_o(g, lax.rem(me + k, n), hg, i).start()
            orecv[hg, pl.ds(pl.multiple_of(tok * i, tok), tok), :] = osend[g, pl.ds(pl.multiple_of(tok * me, tok), tok), :]


    @pl.when(core == 0)
    def _():
        for k in (0, 1, 2, 3, 6, 7, 4, 5):
            s = lax.rem(me + k, n)
            if k:
                send_y(0, 0, s, s).wait_recv()
            forward(s, me + 1).start()
        run_groups((0, 1), 0, pos_full)

    @pl.when(core == 1)
    def _():
        for k in range(1, n):
            s = lax.rem(me + k, n)
            send_y(0, 0, s, s).wait_recv()
        run_groups((0, 1), 0, pos_split)
        forward_all(me - 1).wait_recv()
        run_groups((2, 3), 1, pos_full)

    cp_wo.wait()
    for w in range(2):
        lo, hi = bounds[w], bounds[w + 1]
        rows = slice(tok * lo, tok * hi)
        for hg in (0, 2, 1, 3):
            mine = sum(jnp.where(me == source_of(p, hg), 1, 0) for p in range(lo, hi))
            for k in range(2):
                got = pl.ds(0, tok * (hi - lo - k))

                @pl.when(mine == k)
                def _():
                    pltpu.make_async_remote_copy(
                        osend.at[0, got], orecv.at[hg, got], ossem.at[0], orsem.at[hg, w],
                        device_id={'sp': nxt}, device_id_type=MESH).wait_recv()
            if w == 0:
                res[rows, :] += dot(orecv[hg, rows, :], wo[gw * hg:gw * hg + gw, :])
        if w == 1:
            r = res[rows, :]
            for hg in range(ng):
                r = r + dot(orecv[hg, rows, :], wo[gw * hg:gw * hg + gw, :])
            res[rows, :] = r
        y2[rows, :] = norm(res[rows, :], row(g2), row(be2)).astype(BF16)
        if w == 0:
            cp_w2.wait()
        for c in range(0, ff, 512):
            k = min(512, ff - c)
            h = dot(y2[rows, :], w1t[:, c:c + k]) + b1[pl.ds(c, k)].reshape(1, k)
            hid[rows, c:c + k] = gelu(h).astype(BF16)
        for j in range(0, d, 256):
            k = min(256, d - j)
            acc = res[rows, j:j + k] + dot(hid[rows, :], w2[:, j:j + k])
            acc = (acc + b2[pl.ds(j, k)].reshape(1, k)).astype(BF16)
            for p in range(lo, hi):
                out[tok * order[p]:tok * order[p] + tok, j:j + k] = acc[tok * (p - lo):tok * (p - lo) + tok, :]
            if w == 1:
                pltpu.make_async_copy(out.at[:, pl.ds(j, k)], out_hbm.at[:, pl.ds(j, k)], outsem.at[0]).start()
    wait_sent(1)

    @pl.when(core == 0)
    def _():
        forward_all(me + 1).wait_send()

    def drain(gs):
        rows = pl.ds(0, tok * (n - 1))
        for g in gs:
            pltpu.make_async_remote_copy(
                osend.at[g, rows], osend.at[0, rows], ossem.at[g], orsem.at[0, 0], device_id={'sp': nxt}, device_id_type=MESH).wait_send()

    drain((0, 1))

    @pl.when(core == 1)
    def _():
        drain((2, 3))

    pltpu.make_async_copy(out, out_hbm, outsem.at[0]).wait()


def solution(mesh):
    n = mesh.shape['sp']

    def device_step(images, w_patch, b_patch, pos_embed, ln1_gain, ln1_bias, w_qkv, b_qkv, w_out, b_out, ln2_gain, ln2_bias, w_fc1, b_fc1, w_fc2, b_fc2):
        nimg, rows, width, chans = images.shape
        tok, d = pos_embed.shape
        patch = w_patch.shape[0]
        _, _, heads, hd = w_qkv.shape
        ff = w_fc1.shape[1]
        m = nimg * tok
        ntok = n * tok
        cfg = (n, nimg, tok, d, heads, hd, ff, patch, chans)
        img_t = jnp.transpose(images, (0, 3, 1, 2))
        wp_t = jnp.transpose(w_patch, (0, 2, 1, 3))
        wqkv_t = jnp.transpose(w_qkv, (1, 2, 3, 0)).reshape(3 * d, d)
        wo_t = w_out.reshape(d, d)
        w1_t = jnp.transpose(w_fc1, (1, 0))

        hbm = pl.BlockSpec(memory_space=pltpu.HBM)
        V, S = pltpu.VMEM, pltpu.SemaphoreType.DMA
        out = pl.pallas_call(
            functools.partial(body, cfg),
            out_shape=jax.ShapeDtypeStruct((m, d), BF16),
            in_specs=[hbm] * 16,
            out_specs=hbm,
            scratch_shapes=[
                V((m, d), BF16),
                V(img_t.shape, F32), V(wp_t.shape, BF16), V((chans, 16, 16, d), BF16),
                V((4, 12 * hd, d), BF16), V((d, d), BF16), V((4, 512, d), BF16), V((d, ff), BF16), V((ff, d), BF16),
                V((d,), F32), V((tok, d), BF16), V((d,), F32), V((d,), F32), V((3, heads, hd), F32), V((d,), F32), V((d,), F32),
                V((d,), F32), V((ff,), F32), V((d,), F32),
                V((8 * chans, 16, width), F32), V((4 * tok, chans * 256), BF16),
                V((m, d), BF16), V((m, d), BF16), V((2, ntok, d), BF16),
                V((2, 12 * hd, ntok), F32), V((4, ntok, ntok), F32), V((4, ntok, ntok), BF16),
                V((3, 4, 8, hd), F32), V((4, 3, hd, 8), F32),
                V((4, ntok, 4 * hd), BF16), V((4, m, 4 * hd), BF16), V((m, d), F32), V((m, d), BF16), V((m, ff), BF16),
                S((1,)), S((2,)), S((2,)), S((1,)), S((4,)), S((4,)), S((10,)), S((2,)), S((n,)), S((1,)), S((1,)), S((4,)), S((4, 2)),
            ],
            compiler_params=pltpu.CompilerParams(collective_id=0, has_side_effects=True, vmem_limit_bytes=60 * 1024 * 1024),
            name='siglip_layer',
        )(img_t, wp_t, b_patch, pos_embed, ln1_gain, ln1_bias, wqkv_t, b_qkv, wo_t, b_out,
          ln2_gain, ln2_bias, w1_t, b_fc1, w_fc2, b_fc2)
        return out.reshape(nimg, tok, d)

    in_specs = (P('dp', 'sp', None, None), P(), P(), P('sp', None), P(), P(), P(), P(), P(), P(), P(), P(), P(), P(), P(), P())
    return jax.shard_map(device_step, mesh=mesh, in_specs=in_specs, out_specs=P('dp', 'sp', None), check_vma=False)
```

time: 33 us -> 31 us (0.939)
  Pallas kernels: 31 us -> 29 us
    pallas_call x1, Pallas kernels: 31 us -> 29 us  [device_step(): pl.pallas_call(functools.partial(body, cfg), out_shape=jax.ShapeDtypeStru...]
where the time goes in v4:
time: 31 us; the launch traced here: 30.8 us
  Pallas kernels  29 us (94%)
  local copies, waits for them, and re-layouts  1.81 us (6%)
    pallas_call x1, Pallas kernels, device_step(): pl.pallas_call(functools.partial(body, cfg), out_shape=jax.ShapeDtypeStru...  29 us
    unnamed x1, local copies, waits for them, and re-layouts  1.81 us

profile of v4, /device:TPU:81, one launch (start us, length us, event | category | flops | bytes accessed | tf_op | source)
XLA Modules:
  0.0 30.8 jit_solution(13011131254080307109)
XLA Ops:
  0.0 29.0 %siglip_layer.1 = bf16[192,1152]{1,0:T(8,128)(2,1)} custom-call(f32[6,3,28,224]{3,2,1,0:T(8,128)} %bitcast.13, bf16[14,3,14,1152]{3,2,1,0:T(8,128)(2,1)} %bitcast.12, f32[1152]{0:T(1024)} %refs_2_.1, bf16[32,1152]{1,0:T(8,128)(2,1)} %refs_3_.1, f32[1152]{0:T(1024)} %refs_4_.1, f32[1152]{0:T(1024)} %refs_5_.1, bf16[3456,1152]{1,0:T(8,128)(2,1)} %bitcast.9, ...), custom_call_target="tpu_custom_call" | custom-call | tf_op jit(solution)/shard_map/siglip_layer/pallas_call | solution.py:371
  29.0 1.8 %copy.18 = bf16[6,32,1152]{2,1,0:T(8,128)(2,1)} copy(bf16[6,32,1152]{2,1,0:T(8,128)(2,1)} %bitcast.11) | data formatting | bytes 884736

commit v5 on v4

--- a/solution.py
+++ b/solution.py
@@ -56,7 +56,7 @@
      zf, xs, x0, y1, yrecv, qkv, sbuf, pbuf, bsc, bcol, osend, orecv, res, y2, hid,
      outsem, isem, wsem, psem, qsem, csem, vsem, ssem, rsem, fsem, frsem, ossem, orsem) = refs
     ntok = n * tok
-    gh, ng = 4, 4
+    gh, ng = 4, 3
     step, slots = w1s.shape[1], w1s.shape[0]
     gw = gh * hd
     me = lax.axis_index('sp')
@@ -67,7 +67,7 @@
     order = [i for i in range(nimg) if i % 3 == 1] + [i for i in range(nimg) if i % 3 != 1]
 
     def source_of(p, hg):
-        return 2 * (2 * p + hg // 2) + 1 if p < 2 else 2 * (p - 2) + hg // 2
+        return 2 * (2 * p + hg // 2) + 1 if p < 2 else 2 * (p - 2) + (hg == 0)
 
     def send_y(i, src_row, e, slot):
         return pltpu.make_async_remote_copy(
@@ -101,7 +101,7 @@
             ossem.at[g], orsem.at[hg, wave_of(g)], device_id={'sp': s}, device_id_type=MESH)
 
     def head_group(g):
-        return (1 - core) * g + core * (2 * side + g) if g < 2 else g
+        return (1 - core) * (g + 1) + core * (2 * side + g) if g < 2 else (1 - core) * (g + 1)
 
     def w1_copy(c, slot, size):
         start = c * step if isinstance(c, int) else pl.multiple_of(c * step, step)
@@ -155,7 +155,7 @@
         nb = len(batch)
         pltpu.make_async_copy(img_hbm.at[pl.ds(0, nb)], img.at[pl.ds(0, nb)], isem.at[bi]).wait()
         if bi == len(batches) - 1:
-            for c in cp_q[:6]:
+            for c in cp_q:
                 c.start()
         for b, i in enumerate(batch):
             for y in range(2):
@@ -214,14 +214,11 @@
             bsc[t, hg, 0:gh, :] = bqkv[t, gh * hg:gh * hg + gh, :]
     for g in range(ng):
         for t in range(3):
-            bcol[g, t] = jnp.transpose(bsc[t, head_group(g)])
+            col = jnp.transpose(bsc[t, head_group(g)])
+            for j in range(gh):
+                bcol[g, gw * t + hd * j:gw * t + hd * j + hd, :] = jnp.broadcast_to(col[:, j:j + 1], (hd, 128))
     res[...] = x0[...].astype(F32) + row(bo)
     lax.fori_loop(early, full, turn_step, 0)
-
-    @pl.when(core == 1)
-    def _():
-        for c in cp_q[6:]:
-            c.start()
 
     cp_wo.start()
     cp_w2.start()
@@ -233,36 +230,36 @@
             qkv[g % 2, gw * t:gw * t + gw, :] = dot(wq[g, gw * t:gw * t + gw, :], yrecv[slot], NT)
 
     def head(g, t, j):
-        return qkv[g % 2, gw * t + hd * j:gw * t + hd * j + hd, :] + bcol[g, t, :, j:j + 1]
+        part = slice(gw * t + hd * j, gw * t + hd * j + hd)
+        return qkv[g % 2, part, :] + jnp.concatenate([bcol[g, part, :]] * (ntok // 128), axis=1)
 
     def scores(g, j):
-        sbuf[j] = dot(jnp.transpose(head(g, 1, j)).astype(BF16), head(g, 0, j).astype(BF16))
-
-    def soft(j):
+        sbuf[g % 2, j] = dot(jnp.transpose(head(g, 1, j)).astype(BF16), head(g, 0, j).astype(BF16))
+
+    def soft(g, j):
         for b in range(0, ntok, 128):
-            s = sbuf[j, :, b:b + 128]
+            s = sbuf[g % 2, j, :, b:b + 128]
             p = jnp.exp2((s - jnp.max(s, axis=0, keepdims=True)) * (hd ** -0.5 * LOG2E))
-            pbuf[j, :, b:b + 128] = (p * (1.0 / jnp.sum(p, axis=0, keepdims=True))).astype(BF16)
+            pbuf[g % 2, j, :, b:b + 128] = (p * (1.0 / jnp.sum(p, axis=0, keepdims=True))).astype(BF16)
 
     def mix(g, j):
-        return dot(head(g, 2, j).astype(BF16), pbuf[j])
+        return dot(head(g, 2, j).astype(BF16), pbuf[g % 2, j])
 
     def wait_q(g):
         pltpu.make_async_copy(wqkv_hbm.at[pl.ds(0, 3 * gw)], wq.at[g], qsem.at[g]).wait()
 
     def run_groups(gs, slot, i):
-        wait_q(gs[0])
+        for g in gs:
+            wait_q(g)
         project(gs[0], slot, range(3))
         for g in gs:
-            if g + 1 in gs:
-                wait_q(g + 1)
             for j in range(gh):
                 scores(g, j)
             outs = []
             for j in range(gh):
                 if g + 1 in gs and j < 3:
                     project(g + 1, slot, (j,))
-                soft(j)
+                soft(g, j)
                 if j:
                     outs.append(mix(g, j - 1))
             outs.append(mix(g, gh - 1))
@@ -280,7 +277,7 @@
             if k:
                 send_y(0, 0, s, s).wait_recv()
             forward(s, me + 1).start()
-        run_groups((0, 1), 0, pos_full)
+        run_groups((0, 1, 2), 0, pos_full)
 
     @pl.when(core == 1)
     def _():
@@ -289,36 +286,40 @@
             send_y(0, 0, s, s).wait_recv()
         run_groups((0, 1), 0, pos_split)
         forward_all(me - 1).wait_recv()
-        run_groups((2, 3), 1, pos_full)
+        run_groups((2,), 1, pos_full)
 
     cp_wo.wait()
-    for w in range(2):
+    cp_w2.wait()
+    def recv_o(w, hg):
         lo, hi = bounds[w], bounds[w + 1]
-        rows = slice(tok * lo, tok * hi)
-        for hg in (0, 2, 1, 3):
-            mine = sum(jnp.where(me == source_of(p, hg), 1, 0) for p in range(lo, hi))
-            for k in range(2):
-                got = pl.ds(0, tok * (hi - lo - k))
-
-                @pl.when(mine == k)
-                def _():
-                    pltpu.make_async_remote_copy(
-                        osend.at[0, got], orecv.at[hg, got], ossem.at[0], orsem.at[hg, w],
-                        device_id={'sp': nxt}, device_id_type=MESH).wait_recv()
-            if w == 0:
-                res[rows, :] += dot(orecv[hg, rows, :], wo[gw * hg:gw * hg + gw, :])
-        if w == 1:
-            r = res[rows, :]
-            for hg in range(ng):
-                r = r + dot(orecv[hg, rows, :], wo[gw * hg:gw * hg + gw, :])
-            res[rows, :] = r
+        mine = sum(jnp.where(me == source_of(p, hg), 1, 0) for p in range(lo, hi))
+        for k in range(2):
+            got = pl.ds(0, tok * (hi - lo - k))
+
+            @pl.when(mine == k)
+            def _():
+                pltpu.make_async_remote_copy(
+                    osend.at[0, got], orecv.at[hg, got], ossem.at[0], orsem.at[hg, w],
+                    device_id={'sp': nxt}, device_id_type=MESH).wait_recv()
+
+    def join(w, hgs):
+        rows = slice(tok * bounds[w], tok * bounds[w + 1])
+        r = res[rows, :]
+        for hg in hgs:
+            r = r + dot(orecv[hg, rows, :], wo[gw * hg:gw * hg + gw, :])
+        res[rows, :] = r
+
+    def expand(w):
+        rows = slice(tok * bounds[w], tok * bounds[w + 1])
         y2[rows, :] = norm(res[rows, :], row(g2), row(be2)).astype(BF16)
-        if w == 0:
-            cp_w2.wait()
         for c in range(0, ff, 512):
             k = min(512, ff - c)
             h = dot(y2[rows, :], w1t[:, c:c + k]) + b1[pl.ds(c, k)].reshape(1, k)
             hid[rows, c:c + k] = gelu(h).astype(BF16)
+
+    def contract(w):
+        lo, hi = bounds[w], bounds[w + 1]
+        rows = slice(tok * lo, tok * hi)
         for j in range(0, d, 256):
             k = min(256, d - j)
             acc = res[rows, j:j + k] + dot(hid[rows, :], w2[:, j:j + k])
@@ -327,6 +328,13 @@
                 out[tok * order[p]:tok * order[p] + tok, j:j + k] = acc[tok * (p - lo):tok * (p - lo) + tok, :]
             if w == 1:
                 pltpu.make_async_copy(out.at[:, pl.ds(j, k)], out_hbm.at[:, pl.ds(j, k)], outsem.at[0]).start()
+
+    for w in range(2):
+        for hg in ((0, 2, 1, 3), (1, 0, 2, 3))[w]:
+            recv_o(w, hg)
+        join(w, range(4))
+        expand(w)
+        contract(w)
     wait_sent(1)
 
     @pl.when(core == 0)
@@ -339,11 +347,7 @@
             pltpu.make_async_remote_copy(
                 osend.at[g, rows], osend.at[0, rows], ossem.at[g], orsem.at[0, 0], device_id={'sp': nxt}, device_id_type=MESH).wait_send()
 
-    drain((0, 1))
-
-    @pl.when(core == 1)
-    def _():
-        drain((2, 3))
+    drain(range(ng))
 
     pltpu.make_async_copy(out, out_hbm, outsem.at[0]).wait()
 
@@ -376,15 +380,15 @@
             scratch_shapes=[
                 V((m, d), BF16),
                 V(img_t.shape, F32), V(wp_t.shape, BF16), V((chans, 16, 16, d), BF16),
-                V((4, 12 * hd, d), BF16), V((d, d), BF16), V((4, 512, d), BF16), V((d, ff), BF16), V((ff, d), BF16),
+                V((3, 12 * hd, d), BF16), V((d, d), BF16), V((4, 512, d), BF16), V((d, ff), BF16), V((ff, d), BF16),
                 V((d,), F32), V((tok, d), BF16), V((d,), F32), V((d,), F32), V((3, heads, hd), F32), V((d,), F32), V((d,), F32),
                 V((d,), F32), V((ff,), F32), V((d,), F32),
                 V((8 * chans, 16, width), F32), V((4 * tok, chans * 256), BF16),
                 V((m, d), BF16), V((m, d), BF16), V((2, ntok, d), BF16),
-                V((2, 12 * hd, ntok), F32), V((4, ntok, ntok), F32), V((4, ntok, ntok), BF16),
-                V((3, 4, 8, hd), F32), V((4, 3, hd, 8), F32),
-                V((4, ntok, 4 * hd), BF16), V((4, m, 4 * hd), BF16), V((m, d), F32), V((m, d), BF16), V((m, ff), BF16),
-                S((1,)), S((2,)), S((2,)), S((1,)), S((4,)), S((4,)), S((10,)), S((2,)), S((n,)), S((1,)), S((1,)), S((4,)), S((4, 2)),
+                V((2, 12 * hd, ntok), F32), V((2, 4, ntok, ntok), F32), V((2, 4, ntok, ntok), BF16),
+                V((3, 4, 8, hd), F32), V((3, 12 * hd, 128), F32),
+                V((3, ntok, 4 * hd), BF16), V((4, m, 4 * hd), BF16), V((m, d), F32), V((m, d), BF16), V((m, ff), BF16),
+                S((1,)), S((2,)), S((2,)), S((1,)), S((3,)), S((4,)), S((10,)), S((2,)), S((n,)), S((1,)), S((1,)), S((3,)), S((4, 2)),
             ],
             compiler_params=pltpu.CompilerParams(collective_id=0, has_side_effects=True, vmem_limit_bytes=60 * 1024 * 1024),
             name='siglip_layer',

time: 31 us -> 29.6 us (0.955)
  Pallas kernels: 29 us -> 27.7 us
    pallas_call x1, Pallas kernels: 29 us -> 27.7 us  [device_step(): pl.pallas_call(functools.partial(body, cfg), out_shape=jax.ShapeDtypeStru...]
where the time goes in v5:
time: 29.6 us; the launch traced here: 29.5 us
  Pallas kernels  27.7 us (94%)
  local copies, waits for them, and re-layouts  1.81 us (6%)
    pallas_call x1, Pallas kernels, device_step(): pl.pallas_call(functools.partial(body, cfg), out_shape=jax.ShapeDtypeStru...  27.7 us
    unnamed x1, local copies, waits for them, and re-layouts  1.81 us

profile of v5, /device:TPU:81, one launch (start us, length us, event | category | flops | bytes accessed | tf_op | source)
XLA Modules:
  0.0 29.5 jit_solution(7265973039676236839)
XLA Ops:
  0.0 27.7 %siglip_layer.1 = bf16[192,1152]{1,0:T(8,128)(2,1)} custom-call(f32[6,3,28,224]{3,2,1,0:T(8,128)} %bitcast.13, bf16[14,3,14,1152]{3,2,1,0:T(8,128)(2,1)} %bitcast.12, f32[1152]{0:T(1024)} %refs_2_.1, bf16[32,1152]{1,0:T(8,128)(2,1)} %refs_3_.1, f32[1152]{0:T(1024)} %refs_4_.1, f32[1152]{0:T(1024)} %refs_5_.1, bf16[3456,1152]{1,0:T(8,128)(2,1)} %bitcast.9, ...), custom_call_target="tpu_custom_call" | custom-call | tf_op jit(solution)/shard_map/siglip_layer/pallas_call | solution.py:375
  27.7 1.8 %copy.18 = bf16[6,32,1152]{2,1,0:T(8,128)(2,1)} copy(bf16[6,32,1152]{2,1,0:T(8,128)(2,1)} %bitcast.11) | data formatting | bytes 884736

commit v6 on v5

--- a/solution.py
+++ b/solution.py
@@ -190,7 +190,6 @@
             pl.semaphore_wait(barrier, n - 1)
         if bi == 1:
             lax.fori_loop(0, early, turn_step, 0)
-            wait_sent(0)
         for k in (2, 1, 3, 0):
             c = lax.rem(chip + k, n // 2)
             if bi == 0:
@@ -304,10 +303,8 @@
 
     def join(w, hgs):
         rows = slice(tok * bounds[w], tok * bounds[w + 1])
-        r = res[rows, :]
-        for hg in hgs:
-            r = r + dot(orecv[hg, rows, :], wo[gw * hg:gw * hg + gw, :])
-        res[rows, :] = r
+        o = jnp.concatenate([orecv[hg, rows, :] for hg in hgs], axis=1)
+        res[rows, :] += dot(o, wo[...])
 
     def expand(w):
         rows = slice(tok * bounds[w], tok * bounds[w + 1])
@@ -335,6 +332,7 @@
         join(w, range(4))
         expand(w)
         contract(w)
+    wait_sent(0)
     wait_sent(1)
 
     @pl.when(core == 0)

time: 29.6 us -> 28.9 us (0.976)
  Pallas kernels: 27.7 us -> 26.9 us
    pallas_call x1, Pallas kernels: 27.7 us -> 26.9 us  [device_step(): pl.pallas_call(functools.partial(body, cfg), out_shape=jax.ShapeDtypeStru...]
where the time goes in v6:
time: 28.9 us; the launch traced here: 28.8 us
  Pallas kernels  26.9 us (93%)
  local copies, waits for them, and re-layouts  1.81 us (6%)
    pallas_call x1, Pallas kernels, device_step(): pl.pallas_call(functools.partial(body, cfg), out_shape=jax.ShapeDtypeStru...  26.9 us
    unnamed x1, local copies, waits for them, and re-layouts  1.81 us

profile of v6, /device:TPU:81, one launch (start us, length us, event | category | flops | bytes accessed | tf_op | source)
XLA Modules:
  0.0 28.8 jit_solution(2294172934244811512)
XLA Ops:
  0.0 26.9 %siglip_layer.1 = bf16[192,1152]{1,0:T(8,128)(2,1)} custom-call(f32[6,3,28,224]{3,2,1,0:T(8,128)} %bitcast.13, bf16[14,3,14,1152]{3,2,1,0:T(8,128)(2,1)} %bitcast.12, f32[1152]{0:T(1024)} %refs_2_.1, bf16[32,1152]{1,0:T(8,128)(2,1)} %refs_3_.1, f32[1152]{0:T(1024)} %refs_4_.1, f32[1152]{0:T(1024)} %refs_5_.1, bf16[3456,1152]{1,0:T(8,128)(2,1)} %bitcast.9, ...), custom_call_target="tpu_custom_call" | custom-call | tf_op jit(solution)/shard_map/siglip_layer/pallas_call | solution.py:373
  26.9 1.8 %copy.18 = bf16[6,32,1152]{2,1,0:T(8,128)(2,1)} copy(bf16[6,32,1152]{2,1,0:T(8,128)(2,1)} %bitcast.11) | data formatting | bytes 884736

commit v7 on v6

--- a/solution.py
+++ b/solution.py
@@ -110,7 +110,7 @@
     batches = (order[:2], order[2:])
     bounds = (0, 2, nimg)
     cp_img = [pltpu.make_async_copy(img_hbm.at[i], img.at[i], isem.at[0 if i in order[:2] else 1]) for i in range(nimg)]
-    cp_wp = [pltpu.make_async_copy(wp_hbm, wp_raw, psem.at[0])]
+    cp_wp = [pltpu.make_async_copy(wp_hbm.at[pl.ds(k, 2)], wp_raw.at[pl.ds(k, 2)], psem.at[0]) for k in range(0, patch, 2)]
     cp_wo = pltpu.make_async_copy(wo_hbm, wo, wsem.at[0])
     cp_w2 = pltpu.make_async_copy(w2_hbm, w2, wsem.at[1])
     cp_q = [pltpu.make_async_copy(
@@ -173,7 +173,8 @@
             for c in range(chans):
                 xs[0:nb * tok, 256 * c + 128 * ph:256 * c + 128 * ph + 128] = t[:, c].reshape(nb * tok, 128)
         if bi == 0:
-            for c in cp_wp + cp_v[:4]:
+            pltpu.make_async_copy(wp_hbm, wp_raw, psem.at[0]).wait()
+            for c in cp_v[:4]:
                 c.wait()
             for c in range(slots):
                 w1_copy(c, c, step).start()

time: 28.9 us -> 28.9 us (level)
  no operation moved by 1% of the time
where the time goes in v7:
time: 28.9 us; the launch traced here: 28.8 us
  Pallas kernels  27 us (93%)
  local copies, waits for them, and re-layouts  1.81 us (6%)
    pallas_call x1, Pallas kernels, device_step(): pl.pallas_call(functools.partial(body, cfg), out_shape=jax.ShapeDtypeStru...  27 us
    unnamed x1, local copies, waits for them, and re-layouts  1.81 us

profile of v7, /device:TPU:81, one launch (start us, length us, event | category | flops | bytes accessed | tf_op | source)
XLA Modules:
  0.0 28.8 jit_solution(5765774584947213340)
XLA Ops:
  0.0 27.0 %siglip_layer.1 = bf16[192,1152]{1,0:T(8,128)(2,1)} custom-call(f32[6,3,28,224]{3,2,1,0:T(8,128)} %bitcast.13, bf16[14,3,14,1152]{3,2,1,0:T(8,128)(2,1)} %bitcast.12, f32[1152]{0:T(1024)} %refs_2_.1, bf16[32,1152]{1,0:T(8,128)(2,1)} %refs_3_.1, f32[1152]{0:T(1024)} %refs_4_.1, f32[1152]{0:T(1024)} %refs_5_.1, bf16[3456,1152]{1,0:T(8,128)(2,1)} %bitcast.9, ...), custom_call_target="tpu_custom_call" | custom-call | tf_op jit(solution)/shard_map/siglip_layer/pallas_call | solution.py:374
  27.0 1.8 %copy.18 = bf16[6,32,1152]{2,1,0:T(8,128)(2,1)} copy(bf16[6,32,1152]{2,1,0:T(8,128)(2,1)} %bitcast.11) | data formatting | bytes 884736
